TPU v7x, 512 devices: a 8x2x16 block of a 8x8x16 slice. The times are simulated.
512 devices in a mesh: grp: 2 (over y), leaf: 32 (over z, core), sub: 8 (over x).
Axes of the slice: x: 8, y: 2, z: 16, core: 2. Of those that a mesh axis runs over, the one named last changes fastest.
The devices are a block of a 8x8x16 slice.
Arguments:
- targets: bfloat16 [64, 1048576], P(None, ('grp', 'leaf', 'sub')), parts along dimension 1, may hold values from -6 to 6
- tree_order: int32 [512, 2048], P(('grp', 'leaf', 'sub')), parts along dimension 0, may hold values from 0 to 2047, each once within a row
- leaf_inverse: bfloat16 [2048, 512, 512], P(('grp', 'leaf', 'sub')), parts along dimension 0, as said below
- cluster_basis: bfloat16 [10, 32, 1048576], P(None, None, ('grp', 'leaf', 'sub')), parts along dimension 2, may hold values from -1.5 to 1.5
- coupling: float32 [512, 10, 32, 64], P(('grp', 'leaf', 'sub')), parts along dimension 0, may hold values from -0.75 to 0.75
- train_coords: bfloat16 [3, 1048576], P(None, ('grp', 'leaf', 'sub')), parts along dimension 1, may hold values from 0 to 1
- test_coords: bfloat16 [3, 1048576], P(None, ('grp', 'leaf', 'sub')), parts along dimension 1, may hold values from 0 to 1
- test_basis: bfloat16 [8, 32, 1048576], P(None, None, ('grp', 'leaf', 'sub')), parts along dimension 2, may hold values from -2.4 to 2.4
- near_leaves: int32 [512, 8], P(('grp', 'leaf', 'sub')), parts along dimension 0, may hold values from 0 to 1023, as said below
Outputs:
- posterior_mean: bfloat16 [64, 1048576], P(None, ('grp', 'leaf', 'sub')), parts along dimension 1
There are 2 independent parts, one for each index of `grp`. A program takes and returns all parts, laid end to end along the dimension named above; each array names one. Nothing has to cross between parts.
Inputs may be any that keep to these rules, and one draw needn't show every extreme that they name: `tree_order`: row d is a permutation of the positions 0 to 2047 within panel d. `near_leaves`: row d names 8 different training leaves, all held by panels d - 1, d or d + 1. `leaf_inverse`: each block is the identity plus dense full-rank entries of spread 0.5 / sqrt(512).
All inputs are finite; a program needn't handle non-finite values.
Results may differ from a plain program's by a relative error of at most 0.0035.
Values may be sent and summed in bfloat16 or wider, within the bound.
No kernel may reach another device: no remote copies, remote signals or barrier semaphores. Data moves between devices by JAX's collectives and lax.ppermute only.
A program may use at most 64 MiB of HBM per device.

v0:
```python
import math

import jax
import jax.numpy as jnp
from jax import lax
from jax.experimental import pallas as pl
from jax.experimental.pallas import tpu as pltpu
from jax.sharding import Mesh
from jax.sharding import PartitionSpec as P

length_scale = 0.5
highest = lax.Precision.HIGHEST
low_axes = ("core", "sub")
panel_axes = ("z", "core", "sub")
f32 = jnp.float32
bf16 = jnp.bfloat16
rows_by_columns = (((1,), (0,)), ((), ()))
rows_by_rows = (((1,), (1,)), ((), ()))
columns_by_columns = (((0,), (0,)), ((), ()))


def thirds(value):
    high = value.astype(bf16)
    rest = value - high.astype(f32)
    middle = rest.astype(bf16)
    low = (rest - middle.astype(f32)).astype(bf16)
    return high, middle, low


def wide_dot(left, right, dims):
    rows = left.shape[0]
    stacked = jnp.concatenate(thirds(left), axis=0)
    product = lax.dot_general(stacked, right, dims, preferred_element_type=f32)
    return product[:rows] + product[rows : 2 * rows] + product[2 * rows :]


def full_dot(left, right, dims=rows_by_columns):
    return lax.dot_general(left, right, dims, precision=highest, preferred_element_type=f32)


def whole_call(body, out_shape, name, scalars=0, scratch=()):
    def call(*operands):
        specs = [
            pl.BlockSpec(memory_space=pltpu.SMEM if i < scalars else pltpu.VMEM)
            for i in range(len(operands))
        ]
        single = not isinstance(out_shape, (list, tuple))
        out_specs = pl.BlockSpec(memory_space=pltpu.VMEM)
        return pl.pallas_call(
            body,
            out_shape=out_shape,
            in_specs=specs,
            out_specs=out_specs if single else [out_specs] * len(out_shape),
            scratch_shapes=list(scratch),
            name=name,
        )(*operands)

    return call


def points_body(train_ref, test_ref, left_ref, right_ref, rows_ref, *, scale):
    dims, count = train_ref.shape
    ones = jnp.ones((1, count), f32)
    for ref, out_ref in ((train_ref, left_ref), (test_ref, right_ref)):
        exact = ref[...].astype(f32)
        norms = scale * jnp.sum(exact * exact, axis=0, keepdims=True)
        norms = [piece.astype(f32) for piece in thirds(norms)]
        if out_ref is left_ref:
            rows = [exact[axis : axis + 1] for axis in range(dims)] * 3 + norms + [ones] * 3
        else:
            pieces = [piece.astype(f32) for piece in thirds(-2.0 * scale * exact)]
            rows = [piece[axis : axis + 1] for piece in pieces for axis in range(dims)]
            rows = rows + [ones] * 3 + norms
        rows_ref[...] = jnp.zeros_like(rows_ref)
        for place, row in enumerate(rows):
            rows_ref[place : place + 1, :] = row
        out_ref[...] = rows_ref[...].astype(bf16)


def mixer_body(basis_ref, coupling_ref, out_ref, *, local_levels, part):
    rank = coupling_ref.shape[1]
    width = basis_ref.shape[0] - local_levels * rank
    points = basis_ref.shape[1]
    basis = basis_ref[local_levels * rank :, :]
    gram = lax.dot_general(basis, basis, rows_by_rows, preferred_element_type=f32)
    level = lax.broadcasted_iota(jnp.int32, (1, width), 1) // rank
    gram = gram * (lax.exp2(-0.5 * level.astype(f32)) / math.sqrt(points))
    for depth in range(width // rank):
        piece = gram[depth * rank : (depth + 1) * rank, :]
        product = full_dot(coupling_ref[local_levels + depth], piece, columns_by_columns)
        for half in range(2):
            for block in range(rank // part):
                start = half * rank + block * part
                out_ref[depth * (rank // part) + block, half * part : (half + 1) * part, :] = (
                    product[start : start + part, :]
                )


def local_body(targets_ref, order_ref, inverse_ref, basis_ref, coupling_ref, state_ref, terms_ref):
    columns, points = targets_ref.shape
    leaf_count, leaf_size, _ = inverse_ref.shape
    rank = coupling_ref.shape[1]
    local_levels = leaf_count.bit_length() - 1
    place = lax.broadcasted_iota(jnp.int32, (points, leaf_size), 0)
    for leaf in range(leaf_count):
        lanes = slice(leaf * leaf_size, (leaf + 1) * leaf_size)
        chosen = jnp.where(place == order_ref[:, lanes], 1.0, 0.0).astype(bf16)
        block = jnp.dot(targets_ref[...], chosen, preferred_element_type=f32).astype(bf16)
        state_ref[:, lanes] = lax.dot_general(
            block, inverse_ref[leaf], rows_by_rows, preferred_element_type=f32
        )
    for level in range(local_levels):
        child = leaf_size << level
        count = points // child
        mixers = coupling_ref[level]
        bases = [
            basis_ref[level * rank : (level + 1) * rank, c * child : (c + 1) * child]
            for c in range(count)
        ]
        sums = [
            wide_dot(state_ref[:, c * child : (c + 1) * child], bases[c], rows_by_rows)
            / math.sqrt(child)
            for c in range(count)
        ]
        for c in range(count):
            joined = jnp.concatenate([sums[c], sums[c ^ 1]], axis=1)
            mixed = full_dot(joined, mixers, rows_by_rows)
            lanes = slice(c * child, (c + 1) * child)
            state_ref[:, lanes] = state_ref[:, lanes] - wide_dot(mixed, bases[c], rows_by_columns)
    width = terms_ref.shape[1]
    level = lax.broadcasted_iota(jnp.int32, (1, width), 1) // rank
    scale = lax.exp2(-0.5 * level.astype(f32)) / math.sqrt(points)
    terms_ref[...] = (
        wide_dot(state_ref[...], basis_ref[local_levels * rank :, :], rows_by_rows) * scale
    )


def distance_body(slots_ref, window_ref, test_ref, out_ref):
    leaf = slots_ref[pl.program_id(0)]
    train = window_ref[leaf]
    step = 256
    for start in range(0, test_ref.shape[1], step):
        squared = lax.dot_general(
            train, test_ref[:, start : start + step], columns_by_columns,
            preferred_element_type=f32,
        )
        squared = jnp.maximum(squared, 1e-20)
        scaled = squared * lax.rsqrt(squared)
        out_ref[0, :, start : start + step] = ((1.0 + scaled) * jnp.exp(-scaled)).astype(bf16)


def distance_kernel(slots, window, test_features, name):
    leaves, rows, leaf_size = window.shape
    tests = test_features.shape[1]
    return pl.pallas_call(
        distance_body,
        out_shape=jax.ShapeDtypeStruct((slots.shape[0], leaf_size, tests), bf16),
        grid_spec=pltpu.PrefetchScalarGridSpec(
            num_scalar_prefetch=1,
            grid=(slots.shape[0],),
            in_specs=[
                pl.BlockSpec((leaves, rows, leaf_size), lambda i, s: (0, 0, 0)),
                pl.BlockSpec(test_features.shape, lambda i, s: (0, 0)),
            ],
            out_specs=pl.BlockSpec((1, leaf_size, tests), lambda i, s: (i, 0, 0)),
        ),
        name=name,
    )(slots, window, test_features)


def node_sums(members, levels):
    sums = [members]
    for _ in range(levels):
        last = sums[-1]
        sums.append([last[i] + last[i + 1] for i in range(0, len(last), 2)])
    return sums


def chain_sums(values, position, levels):
    tree = node_sums(values, levels)
    own, sibling = [], []
    for level in range(levels):
        nodes = tree[level]
        mine = position >> level
        first, second = nodes[0], nodes[1]
        for node in range(2, len(nodes), 2):
            here = (mine >> 1) == (node >> 1)
            first = jnp.where(here, nodes[node], first)
            second = jnp.where(here, nodes[node + 1], second)
        right = (mine & 1) == 1
        own.append(jnp.where(right, second, first))
        sibling.append(jnp.where(right, first, second))
    return own, sibling


def operator_body(place_ref, spread_ref, high_ref, out_ref, *, rank):
    low_count, rows, width = spread_ref.shape
    part = rows // 2
    high_count, _, high_width = high_ref.shape
    low_width = width - high_width
    low_levels = low_count.bit_length() - 1
    high_levels = high_count.bit_length() - 1
    row_level = place_ref[0] * part // rank
    lane_level = lax.broadcasted_iota(jnp.int32, (part, width), 1) // rank
    pair_level = jnp.minimum(lane_level, row_level)
    upper = pair_level >= low_levels
    below = lane_level < row_level
    equal = lane_level == row_level
    blank = jnp.zeros((part, low_width), f32)
    trees = []
    highs = []
    for half in range(2):
        rows_here = slice(half * part, (half + 1) * part)
        trees.append(node_sums([spread_ref[p, rows_here, :] for p in range(low_count)], low_levels))
        own, sibling = chain_sums(
            [high_ref[p, rows_here, :] for p in range(high_count)], place_ref[1], high_levels
        )
        picks = []
        for values in (own, sibling):
            pick = values[0]
            for level in range(1, high_levels):
                pick = jnp.where(
                    pair_level[:, low_width:] == low_levels + level, values[level], pick
                )
            picks.append(jnp.concatenate([blank, pick], axis=1))
        highs.append(picks)
    for p in range(low_count):
        own, sibling = [], []
        for half in range(2):
            mine, other = highs[half]
            for level in range(low_levels):
                chosen = pair_level == level
                mine = jnp.where(chosen, trees[half][level][p >> level], mine)
                other = jnp.where(chosen, trees[half][level][(p >> level) ^ 1], other)
            own.append(mine)
            sibling.append(other)
        ahead = own[0] + sibling[1]
        out_ref[p, :part, :] = jnp.where(
            below, sibling[0], jnp.where(equal, sibling[1], ahead)
        )
        out_ref[p, part:, :] = jnp.where(equal, sibling[0], sibling[1])


def operators_of(ref, rank):
    count, rows, width = ref.shape
    part = rows // 2
    first = ref[:, :part, :].reshape(count * part, width)
    second = ref[:, part:, :].reshape(count * part, width)
    row_level = lax.broadcasted_iota(jnp.int32, (width, width), 0) // rank
    lane_level = lax.broadcasted_iota(jnp.int32, (width, width), 1) // rank
    return first, second, lane_level > row_level


def eliminate_body(terms_ref, operators_ref, out_ref, *, rank):
    columns, width = terms_ref.shape
    count, share, _ = out_ref.shape
    first, _, ahead = operators_of(operators_ref, rank)
    feed = jnp.where(ahead, first, 0.0)
    half = width // 2

    def solve(value, square):
        double = full_dot(square, square)
        value = value - full_dot(value, square)
        return value + full_dot(value, double)

    early = solve(terms_ref[:, :half], feed[:half, :half])
    late = terms_ref[:, half:] - full_dot(early, feed[:half, half:])
    late = solve(late, feed[half:, half:])
    for j in range(count):
        rows = slice(j * share, (j + 1) * share)
        out_ref[j, :, :half] = early[rows, :]
        out_ref[j, :, half:] = late[rows, :]


def sums_body(place_ref, spread_ref, high_ref, out_ref, *, rank):
    low_count, share, width = spread_ref.shape
    high_count, _, high_width = high_ref.shape
    low_width = width - high_width
    low_levels = low_count.bit_length() - 1
    high_levels = high_count.bit_length() - 1
    lane_level = lax.broadcasted_iota(jnp.int32, (share, width), 1) // rank
    tree = node_sums([spread_ref[p] for p in range(low_count)], low_levels)
    blank = jnp.zeros((share, low_width), f32)
    highs = []
    for values in chain_sums([high_ref[p] for p in range(high_count)], place_ref[1], high_levels):
        pick = values[0]
        for level in range(1, high_levels):
            pick = jnp.where(lane_level[:, low_width:] == low_levels + level, values[level], pick)
        highs.append(jnp.concatenate([blank, pick], axis=1))
    for p in range(low_count):
        mine, other = highs
        for level in range(low_levels):
            chosen = lane_level == level
            mine = jnp.where(chosen, tree[level][p >> level], mine)
            other = jnp.where(chosen, tree[level][(p >> level) ^ 1], other)
        out_ref[p, :share, :] = mine
        out_ref[p, share:, :] = other


def weights_body(sums_ref, state_ref, basis_ref, coupling_ref, weights_ref, joined_ref, *, local_levels):
    count, rows, width = sums_ref.shape
    share = rows // 2
    columns = count * share
    rank = coupling_ref.shape[1]
    for j in range(count):
        joined_ref[j * share : (j + 1) * share, :] = sums_ref[j, :share, :]
        joined_ref[columns + j * share : columns + (j + 1) * share, :] = sums_ref[j, share:, :]
    pieces = []
    for level in range(width // rank):
        lanes = slice(level * rank, (level + 1) * rank)
        joined = jnp.concatenate(
            [joined_ref[:columns, lanes], joined_ref[columns:, lanes]], axis=1
        )
        pieces.append(full_dot(joined, coupling_ref[local_levels + level], rows_by_rows))
    mixed = jnp.concatenate(pieces, axis=1)
    update = wide_dot(mixed, basis_ref[local_levels * rank :, :], rows_by_columns)
    weights_ref[...] = (state_ref[...] - update).astype(bf16)


def mean_body(
    slots_ref, before_ref, mine_ref, after_ref, early_ref, late_ref, joined_ref, operators_ref,
    test_ref, out_ref, window_ref, near_ref, *, rank, leaf_size, factor,
):
    step = pl.program_id(0)
    steps = pl.num_programs(0)
    columns = mine_ref.shape[0]
    leaf_count = mine_ref.shape[1] // leaf_size

    @pl.when(step == 0)
    def _():
        for side, ref in enumerate((before_ref, mine_ref, after_ref)):
            for leaf in range(leaf_count):
                window_ref[side * leaf_count + leaf] = ref[
                    :, leaf * leaf_size : (leaf + 1) * leaf_size
                ]
        first, second, ahead = operators_of(operators_ref, rank)
        own = joined_ref[:columns, :]
        sibling = joined_ref[columns:, :]
        far = (
            sibling
            - full_dot(own, jnp.where(ahead, 0.0, first))
            - full_dot(sibling, jnp.where(ahead, 0.0, second))
        )
        near_ref[...] = wide_dot(far, test_ref[...], rows_by_columns) / factor

    near_ref[...] += jnp.dot(
        window_ref[slots_ref[step]], early_ref[0], preferred_element_type=f32
    ) + jnp.dot(window_ref[slots_ref[steps + step]], late_ref[0], preferred_element_type=f32)

    @pl.when(step == steps - 1)
    def _():
        out_ref[...] = (near_ref[...] * factor).astype(bf16)


def mean_kernel(slots, before, mine, after, early, late, joined, operators, test, rank, factor):
    steps, leaf_size, tests = early.shape
    columns, points = mine.shape
    whole = [before, mine, after]

    def fixed(array):
        return pl.BlockSpec(array.shape, lambda i, s: (0,) * array.ndim)

    moving = pl.BlockSpec((1, leaf_size, tests), lambda i, s: (i, 0, 0))

    def body(*refs):
        mean_body(*refs, rank=rank, leaf_size=leaf_size, factor=factor)

    return pl.pallas_call(
        body,
        out_shape=jax.ShapeDtypeStruct((columns, tests), bf16),
        grid_spec=pltpu.PrefetchScalarGridSpec(
            num_scalar_prefetch=1,
            grid=(steps,),
            in_specs=[fixed(a) for a in whole]
            + [moving, moving]
            + [fixed(a) for a in (joined, operators, test)],
            out_specs=pl.BlockSpec((columns, tests), lambda i, s: (0, 0)),
            scratch_shapes=[
                pltpu.VMEM((3 * points // leaf_size, columns, leaf_size), bf16),
                pltpu.VMEM((columns, tests), f32),
            ],
        ),
        name="posterior_mean",
    )(slots, *whole, early, late, joined, operators, test)


def exchange(value, axes):
    return lax.all_to_all(value, axes, 0, 0)


def gathered(value, axes):
    count = lax.axis_size(axes)
    return exchange(jnp.broadcast_to(value[None], (count,) + value.shape), axes)


def tie(*values):
    return lax.optimization_barrier(values)


def shards(
    targets,
    tree_order,
    leaf_inverse,
    cluster_basis,
    coupling,
    train_coords,
    test_coords,
    test_basis,
    near_leaves,
):
    columns, points = targets.shape
    leaf_count, leaf_size = leaf_inverse.shape[:2]
    all_levels, rank = cluster_basis.shape[:2]
    local_levels = leaf_count.bit_length() - 1
    low_count = lax.axis_size(low_axes)
    high_count = lax.axis_size("z")
    low_levels = low_count.bit_length() - 1
    low = lax.axis_index(low_axes)
    high = lax.axis_index("z")
    panels = low_count * high_count
    width = (all_levels - local_levels) * rank
    low_width = low_levels * rank
    part = width // low_count
    share = columns // low_count
    place = jnp.stack([low, high]).astype(jnp.int32)
    position = high * low_count + low
    basis = cluster_basis.reshape(all_levels * rank, points)
    mixers = coupling[0]
    half_slots = near_leaves.shape[1] // 2

    def mixer(*refs):
        mixer_body(*refs, local_levels=local_levels, part=part)

    effect = whole_call(
        mixer, jax.ShapeDtypeStruct((low_count, 2 * part, width), f32), "mixer"
    )(basis, mixers)
    spread = exchange(effect, low_axes)

    def featured(*refs):
        points_body(*refs, scale=3.0 / length_scale**2)

    features = jax.ShapeDtypeStruct((16, points), bf16)
    train_rows, test_rows = whole_call(
        featured, [features] * 2, "points", scratch=[pltpu.VMEM((16, points), f32)]
    )(train_coords, test_coords)
    forward = [(i, i + 1) for i in range(panels - 1)]
    backward = [(i + 1, i) for i in range(panels - 1)]
    sides = (
        lax.ppermute(train_rows, panel_axes, forward),
        train_rows,
        lax.ppermute(train_rows, panel_axes, backward),
    )

    state, terms = whole_call(
        local_body,
        [
            jax.ShapeDtypeStruct((columns, points), f32),
            jax.ShapeDtypeStruct((columns, width), f32),
        ],
        "local",
    )(targets, tree_order, leaf_inverse, basis, mixers)
    terms, spread = tie(terms, spread)

    window = jnp.concatenate(
        [rows.reshape(-1, leaf_count, leaf_size).transpose(1, 0, 2) for rows in sides], axis=0
    )
    slots = near_leaves[0] - (position - 1) * leaf_count
    total = jnp.sum(spread, axis=0)[:, low_width:]
    early_slots, total = tie(slots[:half_slots], total)
    high_spread = gathered(total, "z")
    early = distance_kernel(early_slots, window, test_rows, "near_early")
    early, high_spread = tie(early, high_spread)

    def operator(*refs):
        operator_body(*refs, rank=rank)

    operators = whole_call(
        operator, jax.ShapeDtypeStruct((low_count, 2 * part, width), f32), "operator", 1
    )(place, spread, high_spread)
    late_slots, operators = tie(slots[half_slots:], operators)
    operators = exchange(operators, low_axes)
    late = distance_kernel(late_slots, window, test_rows, "near_late")
    late, operators = tie(late, operators)

    def eliminate(*refs):
        eliminate_body(*refs, rank=rank)

    own_terms = whole_call(
        eliminate, jax.ShapeDtypeStruct((low_count, share, width), f32), "eliminate"
    )(terms, operators)
    spread = exchange(own_terms, low_axes)
    high_spread = gathered(jnp.sum(spread, axis=0)[:, low_width:], "z")

    def subtree(*refs):
        sums_body(*refs, rank=rank)

    sums = whole_call(
        subtree, jax.ShapeDtypeStruct((low_count, 2 * share, width), f32), "subtree", 1
    )(place, spread, high_spread)
    sums = exchange(sums, low_axes)

    def weigh(*refs):
        weights_body(*refs, local_levels=local_levels)

    weights, joined = whole_call(
        weigh,
        [
            jax.ShapeDtypeStruct((columns, points), bf16),
            jax.ShapeDtypeStruct((2 * columns, width), f32),
        ],
        "weights",
    )(sums, state, basis, mixers)
    before = lax.ppermute(weights, panel_axes, forward)
    after = lax.ppermute(weights, panel_axes, backward)
    return mean_kernel(
        slots,
        before,
        weights,
        after,
        early,
        late,
        joined,
        operators,
        test_basis.reshape(width, -1),
        rank,
        2.0 / math.sqrt(near_leaves.shape[1] * leaf_size),
    )


def solution(mesh):
    grp, leaf, sub = (mesh.shape[name] for name in ("grp", "leaf", "sub"))
    split = Mesh(mesh.devices.reshape(grp, leaf // 2, 2, sub), ("grp",) + panel_axes)
    every = ("grp",) + panel_axes
    return jax.shard_map(
        shards,
        mesh=split,
        in_specs=(
            P(None, every),
            P(every, None),
            P(every, None, None),
            P(None, None, every),
            P(every, None, None, None),
            P(None, every),
            P(None, every),
            P(None, None, every),
            P(every, None),
        ),
        out_specs=P(None, every),
        check_vma=False,
    )
```

profile of v0, /device:TPU:65, one launch (start us, length us, event | category | flops | bytes accessed | tf_op | source)
XLA Modules:
  0.0 201.3 jit_solution(15574197307704053640)
XLA Ops:
  0.0 3.6 %mixer.1 = f32[16,32,256]{2,1,0:T(8,128)} custom-call(bf16[320,2048]{1,0:T(8,128)(2,1)} %bitcast.32, f32[10,32,64]{2,1,0:T(8,128)} %bitcast.35), custom_call_target="tpu_custom_call" | custom-call | tf_op jit(solution)/shard_map/mixer/pallas_call | solution.py:49
  3.6 44.9 %all-to-all-start = ((f32[16,32,256]{2,1,0:T(8,128)}), f32[16,32,256]{2,1,0:T(8,128)S(1)}, u32[]{:S(2)}, u32[]{:S(2)}) async-start(f32[16,32,256]{2,1,0:T(8,128)} %mixer.1), calls=%async_computation | async-start | bytes 1048576 | tf_op jit(solution)/shard_map/all_to_all | solution.py:388
  48.6 7.8 %local.1 = (f32[64,2048]{1,0:T(8,128)}, f32[64,256]{1,0:T(8,128)}) custom-call(bf16[64,2048]{1,0:T(8,128)(2,1)} %targets_ref.1, s32[1,2048]{1,0:T(1,128)} %order_ref.1, bf16[4,512,512]{2,1,0:T(8,128)(2,1)} %inverse_ref.1, bf16[320,2048]{1,0:T(8,128)(2,1)} %bitcast.33, f32[10,32,64]{2,1,0:T(8,128)} %bitcast.36), custom_call_target="tpu_custom_call" | custom-call | tf_op jit(solution)/shard_map/local/pallas_call | solution.py:49
  56.3 0.7 broadcast_subtract_fusion
  57.0 0.6 slice_bitcast_fusion
  57.6 5.8 %all-to-all-done.refs_1_ = f32[16,32,256]{2,1,0:T(8,128)S(1)} async-done(((f32[16,32,256]{2,1,0:T(8,128)}), f32[16,32,256]{2,1,0:T(8,128)S(1)}, u32[]{:S(2)}, u32[]{:S(2)}) %all-to-all-start) | async-done | bytes 524320 | tf_op jit(solution)/shard_map/all_to_all | solution.py:388
  63.3 0.0 copy-start
  63.4 0.9 broadcast_in_dim.4
  64.3 7.2 %all-to-all-start.1 = ((f32[16,32,128]{2,1,0:T(8,128)}), f32[16,32,128]{2,1,0:T(8,128)S(1)}, u32[]{:S(2)}, u32[]{:S(2)}) async-start(f32[16,32,128]{2,1,0:T(8,128)} %broadcast_in_dim.4), calls=%async_computation.1 | async-start | bytes 524288 | tf_op jit(solution)/shard_map/all_to_all | solution.py:388
  71.5 1.5 points.1
  73.0 4.1 %collective-permute-start.1 = (bf16[16,2048]{1,0:T(8,128)(2,1)}, bf16[16,2048]{1,0:T(8,128)(2,1)S(1)}, u32[]{:S(2)}, u32[]{:S(2)}) collective-permute-start(bf16[16,2048]{1,0:T(8,128)(2,1)} %get-tuple-element.25), channel_id=1, source_target_pairs={{1,0},{2,1},{3,2},{4,3},{5,4},{6,5},{7,6},{8,7},{9,8},{10,9},{11,1... | collective-permute-start | bytes 196616 | tf_op jit(solution)/shard_map/ppermute | solution.py:451
  77.1 2.0 collective-permute-start
  79.0 0.9 copy.20
  79.9 0.7 pad_add_fusion.refs_0_
  80.6 0.0 collective-permute-done.1
  80.6 3.8 %collective-permute-done = bf16[16,2048]{1,0:T(8,128)(2,1)S(1)} collective-permute-done((bf16[16,2048]{1,0:T(8,128)(2,1)}, bf16[16,2048]{1,0:T(8,128)(2,1)S(1)}, u32[]{:S(2)}, u32[]{:S(2)}) %collective-permute-start) | collective-permute-done | bytes 65568 | tf_op jit(solution)/shard_map/ppermute | solution.py:449
  84.4 0.7 pad_maximum_fusion.window_ref
  85.1 9.2 %near_early.1.refs_4_ = bf16[4,512,2048]{2,1,0:T(8,128)(2,1)} custom-call(s32[4]{0:T(128)} %get-tuple-element.24.slots_ref, bf16[12,16,512]{2,1,0:T(8,128)(2,1)} %pad_maximum_fusion.window_ref, bf16[16,2048]{1,0:T(8,128)(2,1)} %get-tuple-element.26.test_ref), custom_call_target="tpu_custom_call" | custom-call | tf_op jit(solution)/shard_map/near_early/pallas_call | solution.py:155
  94.4 0.0 copy-start.6
  94.4 0.0 all-to-all-done.1.refs_2_
  94.4 0.0 copy-done
  94.4 0.0 copy-start.2
  94.4 0.7 copy-done.2
  95.1 2.2 %operator.1 = f32[16,32,256]{2,1,0:T(8,128)} custom-call(s32[2]{0:T(128)} %pad_add_fusion.refs_0_, f32[16,32,256]{2,1,0:T(8,128)} %copy-done, f32[16,32,128]{2,1,0:T(8,128)} %copy-done.2), custom_call_target="tpu_custom_call" | custom-call | tf_op jit(solution)/shard_map/operator/pallas_call | solution.py:49
  97.4 6.5 %all-to-all-start.2 = ((f32[16,32,256]{2,1,0:T(8,128)}), f32[16,32,256]{2,1,0:T(8,128)S(1)}, u32[]{:S(2)}, u32[]{:S(2)}) async-start(f32[16,32,256]{2,1,0:T(8,128)} %operator.1), calls=%async_computation.2 | async-start | bytes 1048576 | tf_op jit(solution)/shard_map/all_to_all | solution.py:388
  103.8 9.2 %near_late.1.refs_5_ = bf16[4,512,2048]{2,1,0:T(8,128)(2,1)} custom-call(s32[4]{0:T(128)} %get-tuple-element.29.slots_ref, bf16[12,16,512]{2,1,0:T(8,128)(2,1)} %pad_maximum_fusion.window_ref, bf16[16,2048]{1,0:T(8,128)(2,1)} %get-tuple-element.26.test_ref), custom_call_target="tpu_custom_call" | custom-call | tf_op jit(solution)/shard_map/near_late/pallas_call | solution.py:155
  113.0 5.6 %all-to-all-done.2.refs_1_.refs_7_ = f32[16,32,256]{2,1,0:T(8,128)S(1)} async-done(((f32[16,32,256]{2,1,0:T(8,128)}), f32[16,32,256]{2,1,0:T(8,128)S(1)}, u32[]{:S(2)}, u32[]{:S(2)}) %all-to-all-start.2) | async-done | bytes 524320 | tf_op jit(solution)/shard_map/all_to_all | solution.py:388
  118.6 0.0 copy-start.1
  118.6 0.8 copy-done.1
  119.4 2.8 %eliminate.1 = f32[16,4,256]{2,1,0:T(4,128)} custom-call(f32[64,256]{1,0:T(8,128)} %get-tuple-element.22.refs_0_, f32[16,32,256]{2,1,0:T(8,128)} %copy-done.1), custom_call_target="tpu_custom_call" | custom-call | tf_op jit(solution)/shard_map/eliminate/pallas_call | solution.py:49
  122.2 12.6 %all_to_all.30.refs_1_ = f32[16,4,256]{2,1,0:T(4,128)S(1)} all-to-all(f32[16,4,256]{2,1,0:T(4,128)} %eliminate.1), channel_id=1, replica_groups=mesh['grp'=2,'z'=16,'core'=2,'sub'=8] {'core','sub'}, dimensions={0} | all-to-all | bytes 131072 | tf_op jit(solution)/shard_map/all_to_all | solution.py:388
  134.7 0.0 copy-start.3
  134.8 23.3 %all_to_all.31.refs_2_ = f32[16,4,128]{2,1,0:T(4,128)} all-to-all(f32[16,4,128]{2,1,0:T(4,128)S(1)} %broadcast_in_dim.5), channel_id=1, replica_groups=mesh['grp'=2,'z'=16,'core'=2,'sub'=8] {'z'}, dimensions={0} | all-to-all | bytes 65536 | tf_op jit(solution)/shard_map/all_to_all | solution.py:388
  158.1 0.0 copy-done.3
  158.1 1.5 subtree.1
  159.7 13.7 %all_to_all.32.refs_0_ = f32[16,8,256]{2,1,0:T(8,128)} all-to-all(f32[16,8,256]{2,1,0:T(8,128)} %subtree.1), channel_id=1, replica_groups=mesh['grp'=2,'z'=16,'core'=2,'sub'=8] {'core','sub'}, dimensions={0} | all-to-all | bytes 262144 | tf_op jit(solution)/shard_map/all_to_all | solution.py:388
  173.4 3.1 %weights.1 = (bf16[64,2048]{1,0:T(8,128)(2,1)}, f32[128,256]{1,0:T(8,128)}) custom-call(f32[16,8,256]{2,1,0:T(8,128)} %all_to_all.32.refs_0_, f32[64,2048]{1,0:T(8,128)} %get-tuple-element.32.refs_1_, bf16[320,2048]{1,0:T(8,128)(2,1)} %bitcast.34, f32[10,32,64]{2,1,0:T(8,128)} %bitcast.37), custom_call_target="tpu_custom_call" | custom-call | tf_op jit(solution)/shard_map/weights/pallas_call | solution.py:49
  176.5 4.4 %collective-permute-start.3 = (bf16[64,2048]{1,0:T(8,128)(2,1)}, bf16[64,2048]{1,0:T(8,128)(2,1)S(1)}, u32[]{:S(2)}, u32[]{:S(2)}) collective-permute-start(bf16[64,2048]{1,0:T(8,128)(2,1)} %get-tuple-element.33.refs_2_), channel_id=1, source_target_pairs={{1,0},{2,1},{3,2},{4,3},{5,4},{6,5},{7,6},{8,7},{9,8},{10,9},{11,1... | collective-permute-start | bytes 786440 | tf_op jit(solution)/shard_map/ppermute | solution.py:514
  180.9 2.0 collective-permute-start.2
  182.9 0.0 copy-done.6
  182.9 0.6 fusion.refs_0_
  183.4 3.9 %collective-permute-done.3.refs_3_ = bf16[64,2048]{1,0:T(8,128)(2,1)S(1)} collective-permute-done((bf16[64,2048]{1,0:T(8,128)(2,1)}, bf16[64,2048]{1,0:T(8,128)(2,1)S(1)}, u32[]{:S(2)}, u32[]{:S(2)}) %collective-permute-start.3) | collective-permute-done | bytes 262176 | tf_op jit(solution)/shard_map/ppermute | solution.py:514
  187.3 0.0 copy-start.4
  187.3 2.7 %collective-permute-done.2.refs_1_ = bf16[64,2048]{1,0:T(8,128)(2,1)S(1)} collective-permute-done((bf16[64,2048]{1,0:T(8,128)(2,1)}, bf16[64,2048]{1,0:T(8,128)(2,1)S(1)}, u32[]{:S(2)}, u32[]{:S(2)}) %collective-permute-start.2) | collective-permute-done | bytes 262176 | tf_op jit(solution)/shard_map/ppermute | solution.py:513
  190.0 0.0 copy-start.5
  190.0 0.0 copy-done.4
  190.0 0.7 copy-done.5
  190.7 10.5 %posterior_mean.1 = bf16[64,2048]{1,0:T(8,128)(2,1)} custom-call(s32[8]{0:T(128)} %fusion.refs_0_, bf16[64,2048]{1,0:T(8,128)(2,1)} %copy-done.5, bf16[64,2048]{1,0:T(8,128)(2,1)} %get-tuple-element.33.refs_2_, bf16[64,2048]{1,0:T(8,128)(2,1)} %copy-done.4, bf16[4,512,2048]{2,1,0:T(8,128)(2,1)} %near_early.1.refs_4_, ...), custom_call_target="tpu_custom_call" | custom-call | tf_op jit(solution)/shard_map/posterior_mean/pallas_call | solution.py:368
  (7 shorter events, 0.1 us)
Async XLA Ops:
  3.6 59.7 %all-to-all-start = ((f32[16,32,256]{2,1,0:T(8,128)}), f32[16,32,256]{2,1,0:T(8,128)S(1)}, u32[]{:S(2)}, u32[]{:S(2)}) async-start(f32[16,32,256]{2,1,0:T(8,128)} %mixer.1), calls=%async_computation | async-start | bytes 1048576 | tf_op jit(solution)/shard_map/all_to_all | solution.py:388
  63.3 31.0 %copy-start = (f32[16,32,256]{2,1,0:T(8,128)}, f32[16,32,256]{2,1,0:T(8,128)S(1)}, u32[]{:S(2)}) copy-start(f32[16,32,256]{2,1,0:T(8,128)S(1)} %all-to-all-done.refs_1_) | copy-start | bytes 1572868
  64.3 30.1 %all-to-all-start.1 = ((f32[16,32,128]{2,1,0:T(8,128)}), f32[16,32,128]{2,1,0:T(8,128)S(1)}, u32[]{:S(2)}, u32[]{:S(2)}) async-start(f32[16,32,128]{2,1,0:T(8,128)} %broadcast_in_dim.4), calls=%async_computation.1 | async-start | bytes 524288 | tf_op jit(solution)/shard_map/all_to_all | solution.py:388
  73.0 7.6 %collective-permute-start.1 = (bf16[16,2048]{1,0:T(8,128)(2,1)}, bf16[16,2048]{1,0:T(8,128)(2,1)S(1)}, u32[]{:S(2)}, u32[]{:S(2)}) collective-permute-start(bf16[16,2048]{1,0:T(8,128)(2,1)} %get-tuple-element.25), channel_id=1, source_target_pairs={{1,0},{2,1},{3,2},{4,3},{5,4},{6,5},{7,6},{8,7},{9,8},{10,9},{11,1... | collective-permute-start | bytes 196616 | tf_op jit(solution)/shard_map/ppermute | solution.py:451
  77.1 7.3 %collective-permute-start = (bf16[16,2048]{1,0:T(8,128)(2,1)}, bf16[16,2048]{1,0:T(8,128)(2,1)S(1)}, u32[]{:S(2)}, u32[]{:S(2)}) collective-permute-start(bf16[16,2048]{1,0:T(8,128)(2,1)} %get-tuple-element.25), channel_id=1, source_target_pairs={{0,1},{1,2},{2,3},{3,4},{4,5},{5,6},{6,7},{7,8},{8,9},{9,10},{10,1... | collective-permute-start | bytes 196616 | tf_op jit(solution)/shard_map/ppermute | solution.py:449
  94.4 88.5 %copy-start.6 = (s32[1,8]{1,0:T(1,128)S(1)}, s32[1,8]{1,0:T(1,128)}, u32[]{:S(2)}) copy-start(s32[1,8]{1,0:T(1,128)} %param.17) | copy-start | bytes 100
  94.4 0.7 copy-start.2
  97.4 21.3 %all-to-all-start.2 = ((f32[16,32,256]{2,1,0:T(8,128)}), f32[16,32,256]{2,1,0:T(8,128)S(1)}, u32[]{:S(2)}, u32[]{:S(2)}) async-start(f32[16,32,256]{2,1,0:T(8,128)} %operator.1), calls=%async_computation.2 | async-start | bytes 1048576 | tf_op jit(solution)/shard_map/all_to_all | solution.py:388
  118.6 0.8 copy-start.1
  134.7 23.4 %copy-start.3 = (f32[16,4,256]{2,1,0:T(4,128)}, f32[16,4,256]{2,1,0:T(4,128)S(1)}, u32[]{:S(2)}) copy-start(f32[16,4,256]{2,1,0:T(4,128)S(1)} %all_to_all.30.refs_1_) | copy-start | bytes 196612
  176.5 10.8 %collective-permute-start.3 = (bf16[64,2048]{1,0:T(8,128)(2,1)}, bf16[64,2048]{1,0:T(8,128)(2,1)S(1)}, u32[]{:S(2)}, u32[]{:S(2)}) collective-permute-start(bf16[64,2048]{1,0:T(8,128)(2,1)} %get-tuple-element.33.refs_2_), channel_id=1, source_target_pairs={{1,0},{2,1},{3,2},{4,3},{5,4},{6,5},{7,6},{8,7},{9,8},{10,9},{11,1... | collective-permute-start | bytes 786440 | tf_op jit(solution)/shard_map/ppermute | solution.py:514
  180.9 9.1 %collective-permute-start.2 = (bf16[64,2048]{1,0:T(8,128)(2,1)}, bf16[64,2048]{1,0:T(8,128)(2,1)S(1)}, u32[]{:S(2)}, u32[]{:S(2)}) collective-permute-start(bf16[64,2048]{1,0:T(8,128)(2,1)} %get-tuple-element.33.refs_2_), channel_id=1, source_target_pairs={{0,1},{1,2},{2,3},{3,4},{4,5},{5,6},{6,7},{7,8},{8,9},{9,10},{10,1... | collective-permute-start | bytes 786440 | tf_op jit(solution)/shard_map/ppermute | solution.py:513
  187.3 2.7 %copy-start.4 = (bf16[64,2048]{1,0:T(8,128)(2,1)}, bf16[64,2048]{1,0:T(8,128)(2,1)S(1)}, u32[]{:S(2)}) copy-start(bf16[64,2048]{1,0:T(8,128)(2,1)S(1)} %collective-permute-done.3.refs_3_) | copy-start | bytes 786436
  190.0 0.7 copy-start.5
where the time goes:
time: 202 us; the launch traced here: 201 us
  starting transfers between devices  71 us (35%)
  Pallas kernels  51.5 us (25%)
  blocking collectives  49.6 us (25%)
  waiting for transfers between devices  21.8 us (11%)
  local copies, waits for them, and re-layouts  4.52 us (2%)
  other arithmetic  2.68 us (1%)
    all_to_all x3, starting transfers between devices, exchange(): return lax.all_to_all(value, axes, 0, 0)  58.6 us
    all_to_all x3, blocking collectives, exchange(): return lax.all_to_all(value, axes, 0, 0)  49.6 us
    pallas_call x7, Pallas kernels, call(): pl.pallas_call(body, out_shape=out_shape, in_specs=specs, out_specs=out_s...  22.6 us
    pallas_call x2, Pallas kernels, distance_kernel(): pl.pallas_call(distance_body, out_shape=jax.ShapeDtypeStruct((slots.shape...  18.5 us
    all_to_all x3, waiting for transfers between devices, exchange(): return lax.all_to_all(value, axes, 0, 0)  11.3 us
    pallas_call x1, Pallas kernels, mean_kernel(): pl.pallas_call(body, out_shape=jax.ShapeDtypeStruct((columns, tests), bf1...  10.5 us
    ppermute x1, starting transfers between devices, shards(): after = lax.ppermute(weights, panel_axes, backward)  4.41 us
    ppermute x1, starting transfers between devices, shards(): lax.ppermute(train_rows, panel_axes, backward)  4.11 us
  transfers between devices with their start and end apart: 7, of which 5 were waited for; matrix products, arithmetic and copies ran while one was open for 2% of the time, Pallas kernels for 14%

commit v1 on v0

--- a/solution.py
+++ b/solution.py
@@ -53,6 +53,7 @@
             out_specs=out_specs if single else [out_specs] * len(out_shape),
             scratch_shapes=list(scratch),
             name=name,
+            compiler_params=pltpu.CompilerParams(vmem_limit_bytes=20 << 20),
         )(*operands)
 
     return call
@@ -135,9 +136,18 @@
     )
 
 
-def distance_body(slots_ref, window_ref, test_ref, out_ref):
+def distance_body(slots_ref, before_ref, mine_ref, after_ref, test_ref, out_ref, train_ref):
     leaf = slots_ref[pl.program_id(0)]
-    train = window_ref[leaf]
+    leaf_size = train_ref.shape[1]
+    leaf_count = mine_ref.shape[1] // leaf_size
+    for side, ref in enumerate((before_ref, mine_ref, after_ref)):
+
+        @pl.when(leaf // leaf_count == side)
+        def _(ref=ref):
+            start = pl.multiple_of((leaf % leaf_count) * leaf_size, leaf_size)
+            train_ref[...] = ref[:, pl.ds(start, leaf_size)]
+
+    train = train_ref[...]
     step = 256
     for start in range(0, test_ref.shape[1], step):
         squared = lax.dot_general(
@@ -149,23 +159,22 @@
         out_ref[0, :, start : start + step] = ((1.0 + scaled) * jnp.exp(-scaled)).astype(bf16)
 
 
-def distance_kernel(slots, window, test_features, name):
-    leaves, rows, leaf_size = window.shape
+def distance_kernel(slots, sides, test_features, leaf_size, name):
     tests = test_features.shape[1]
+    operands = (*sides, test_features)
     return pl.pallas_call(
         distance_body,
-        out_shape=jax.ShapeDtypeStruct((slots.shape[0], leaf_size, tests), bf16),
+        out_shape=pltpu.HBM((slots.shape[0], leaf_size, tests), bf16),
         grid_spec=pltpu.PrefetchScalarGridSpec(
             num_scalar_prefetch=1,
             grid=(slots.shape[0],),
-            in_specs=[
-                pl.BlockSpec((leaves, rows, leaf_size), lambda i, s: (0, 0, 0)),
-                pl.BlockSpec(test_features.shape, lambda i, s: (0, 0)),
-            ],
+            in_specs=[pl.BlockSpec(a.shape, lambda i, s: (0, 0)) for a in operands],
             out_specs=pl.BlockSpec((1, leaf_size, tests), lambda i, s: (i, 0, 0)),
+            scratch_shapes=[pltpu.VMEM((sides[0].shape[0], leaf_size), bf16)],
         ),
+        compiler_params=pltpu.CompilerParams(vmem_limit_bytes=24 << 20),
         name=name,
-    )(slots, window, test_features)
+    )(slots, *operands)
 
 
 def node_sums(members, levels):
@@ -235,17 +244,21 @@
             own.append(mine)
             sibling.append(other)
         ahead = own[0] + sibling[1]
-        out_ref[p, :part, :] = jnp.where(
-            below, sibling[0], jnp.where(equal, sibling[1], ahead)
-        )
-        out_ref[p, part:, :] = jnp.where(equal, sibling[0], sibling[1])
+        first = jnp.where(below, sibling[0], jnp.where(equal, sibling[1], ahead))
+        high = first.astype(bf16)
+        out_ref[p, :part, :] = high
+        out_ref[p, part : 2 * part, :] = (first - high.astype(f32)).astype(bf16)
+        out_ref[p, 2 * part :, :] = jnp.where(equal, sibling[0], sibling[1]).astype(bf16)
 
 
 def operators_of(ref, rank):
     count, rows, width = ref.shape
-    part = rows // 2
-    first = ref[:, :part, :].reshape(count * part, width)
-    second = ref[:, part:, :].reshape(count * part, width)
+    part = rows // 3
+    first, rest, second = (
+        ref[:, i * part : (i + 1) * part, :].reshape(count * part, width).astype(f32)
+        for i in range(3)
+    )
+    first = first + rest
     row_level = lax.broadcasted_iota(jnp.int32, (width, width), 0) // rank
     lane_level = lax.broadcasted_iota(jnp.int32, (width, width), 1) // rank
     return first, second, lane_level > row_level
@@ -317,9 +330,22 @@
     weights_ref[...] = (state_ref[...] - update).astype(bf16)
 
 
+def far_body(joined_ref, operators_ref, test_ref, out_ref, *, rank, factor):
+    columns = out_ref.shape[0]
+    first, second, ahead = operators_of(operators_ref, rank)
+    own = joined_ref[:columns, :]
+    sibling = joined_ref[columns:, :]
+    far = (
+        sibling
+        - full_dot(own, jnp.where(ahead, 0.0, first))
+        - full_dot(sibling, jnp.where(ahead, 0.0, second))
+    )
+    out_ref[...] = wide_dot(far, test_ref[...], rows_by_columns) / factor
+
+
 def mean_body(
-    slots_ref, before_ref, mine_ref, after_ref, early_ref, late_ref, joined_ref, operators_ref,
-    test_ref, out_ref, window_ref, near_ref, *, rank, leaf_size, factor,
+    slots_ref, before_ref, mine_ref, after_ref, early_ref, late_ref, far_ref,
+    out_ref, window_ref, near_ref, *, leaf_size, factor,
 ):
     step = pl.program_id(0)
     steps = pl.num_programs(0)
@@ -333,15 +359,7 @@
                 window_ref[side * leaf_count + leaf] = ref[
                     :, leaf * leaf_size : (leaf + 1) * leaf_size
                 ]
-        first, second, ahead = operators_of(operators_ref, rank)
-        own = joined_ref[:columns, :]
-        sibling = joined_ref[columns:, :]
-        far = (
-            sibling
-            - full_dot(own, jnp.where(ahead, 0.0, first))
-            - full_dot(sibling, jnp.where(ahead, 0.0, second))
-        )
-        near_ref[...] = wide_dot(far, test_ref[...], rows_by_columns) / factor
+        near_ref[...] = far_ref[...]
 
     near_ref[...] += jnp.dot(
         window_ref[slots_ref[step]], early_ref[0], preferred_element_type=f32
@@ -352,7 +370,11 @@
         out_ref[...] = (near_ref[...] * factor).astype(bf16)
 
 
-def mean_kernel(slots, before, mine, after, early, late, joined, operators, test, rank, factor):
+def in_hbm(value):
+    return pltpu.with_memory_space_constraint(value, pltpu.HBM)
+
+
+def mean_kernel(slots, before, mine, after, early, late, far, factor):
     steps, leaf_size, tests = early.shape
     columns, points = mine.shape
     whole = [before, mine, after]
@@ -363,7 +385,7 @@
     moving = pl.BlockSpec((1, leaf_size, tests), lambda i, s: (i, 0, 0))
 
     def body(*refs):
-        mean_body(*refs, rank=rank, leaf_size=leaf_size, factor=factor)
+        mean_body(*refs, leaf_size=leaf_size, factor=factor)
 
     return pl.pallas_call(
         body,
@@ -373,15 +395,16 @@
             grid=(steps,),
             in_specs=[fixed(a) for a in whole]
             + [moving, moving]
-            + [fixed(a) for a in (joined, operators, test)],
+            + [fixed(far)],
             out_specs=pl.BlockSpec((columns, tests), lambda i, s: (0, 0)),
             scratch_shapes=[
                 pltpu.VMEM((3 * points // leaf_size, columns, leaf_size), bf16),
                 pltpu.VMEM((columns, tests), f32),
             ],
         ),
+        compiler_params=pltpu.CompilerParams(vmem_limit_bytes=24 << 20),
         name="posterior_mean",
-    )(slots, *whole, early, late, joined, operators, test)
+    )(slots, *whole, in_hbm(early), in_hbm(late), far)
 
 
 def exchange(value, axes):
@@ -434,6 +457,7 @@
     effect = whole_call(
         mixer, jax.ShapeDtypeStruct((low_count, 2 * part, width), f32), "mixer"
     )(basis, mixers)
+    effect, train_coords = tie(effect, train_coords)
     spread = exchange(effect, low_axes)
 
     def featured(*refs):
@@ -450,6 +474,7 @@
         train_rows,
         lax.ppermute(train_rows, panel_axes, backward),
     )
+    *sides, tree_order = tie(*sides, tree_order)
 
     state, terms = whole_call(
         local_body,
@@ -461,25 +486,22 @@
     )(targets, tree_order, leaf_inverse, basis, mixers)
     terms, spread = tie(terms, spread)
 
-    window = jnp.concatenate(
-        [rows.reshape(-1, leaf_count, leaf_size).transpose(1, 0, 2) for rows in sides], axis=0
-    )
     slots = near_leaves[0] - (position - 1) * leaf_count
     total = jnp.sum(spread, axis=0)[:, low_width:]
     early_slots, total = tie(slots[:half_slots], total)
     high_spread = gathered(total, "z")
-    early = distance_kernel(early_slots, window, test_rows, "near_early")
+    early = distance_kernel(early_slots, sides, test_rows, leaf_size, "near_early")
     early, high_spread = tie(early, high_spread)
 
     def operator(*refs):
         operator_body(*refs, rank=rank)
 
     operators = whole_call(
-        operator, jax.ShapeDtypeStruct((low_count, 2 * part, width), f32), "operator", 1
+        operator, jax.ShapeDtypeStruct((low_count, 3 * part, width), bf16), "operator", 1
     )(place, spread, high_spread)
     late_slots, operators = tie(slots[half_slots:], operators)
     operators = exchange(operators, low_axes)
-    late = distance_kernel(late_slots, window, test_rows, "near_late")
+    late = distance_kernel(late_slots, sides, test_rows, leaf_size, "near_late")
     late, operators = tie(late, operators)
 
     def eliminate(*refs):
@@ -512,19 +534,15 @@
     )(sums, state, basis, mixers)
     before = lax.ppermute(weights, panel_axes, forward)
     after = lax.ppermute(weights, panel_axes, backward)
-    return mean_kernel(
-        slots,
-        before,
-        weights,
-        after,
-        early,
-        late,
-        joined,
-        operators,
-        test_basis.reshape(width, -1),
-        rank,
-        2.0 / math.sqrt(near_leaves.shape[1] * leaf_size),
+    factor = 2.0 / math.sqrt(near_leaves.shape[1] * leaf_size)
+
+    def distant(*refs):
+        far_body(*refs, rank=rank, factor=factor)
+
+    far = whole_call(distant, jax.ShapeDtypeStruct((columns, points), f32), "far")(
+        joined, operators, test_basis.reshape(width, -1)
     )
+    return mean_kernel(slots, before, weights, after, early, late, far, factor)
 
 
 def solution(mesh):

time: 202 us -> 191 us (0.946)
  Pallas kernels: 51.5 us -> 38 us
  blocking collectives: 49.6 us -> 40.9 us
  local copies, waits for them, and re-layouts: 4.52 us -> 12.7 us
  starting transfers between devices: 71 us -> 74.4 us
    pallas_call x7 -> x8, Pallas kernels: 22.6 us -> 12.4 us  [call(): pl.pallas_call(body, out_shape=out_shape, in_specs=specs, out_specs=out_s...]
    unnamed x14 -> x38, local copies, waits for them, and re-layouts: 2.21 us -> 11.8 us
    all_to_all x3, blocking collectives: 49.6 us -> 40.9 us  [exchange(): return lax.all_to_all(value, axes, 0, 0)]
    ppermute x1, waiting for transfers between devices: 0.01 us -> 5.95 us  [shards(): lax.ppermute(train_rows, panel_axes, backward)]
    ppermute x1, waiting for transfers between devices: 3.84 us -> 0.75 us  [shards(): lax.ppermute(train_rows, panel_axes, forward)]
    all_to_all x3, starting transfers between devices: 58.6 us -> 61.3 us  [exchange(): return lax.all_to_all(value, axes, 0, 0)]
  transfers between devices with their start and end apart: 7 -> 7, of which waited for: 5 -> 6; matrix products, arithmetic and copies ran while one was open for 2% -> 0% of each run, Pallas kernels for 14% -> 12%
where the time goes in v1:
time: 191 us; the launch traced here: 190 us
  starting transfers between devices  74.4 us (39%)
  blocking collectives  40.9 us (21%)
  Pallas kernels  38 us (20%)
  waiting for transfers between devices  23.1 us (12%)
  local copies, waits for them, and re-layouts  12.7 us (7%)
    all_to_all x3, starting transfers between devices, exchange(): return lax.all_to_all(value, axes, 0, 0)  61.3 us
    all_to_all x3, blocking collectives, exchange(): return lax.all_to_all(value, axes, 0, 0)  40.9 us
    pallas_call x2, Pallas kernels, distance_kernel(): pl.pallas_call(distance_body, out_shape=pltpu.HBM((slots.shape[0], leaf_s...  16.6 us
    pallas_call x8, Pallas kernels, call(): pl.pallas_call(body, out_shape=out_shape, in_specs=specs, out_specs=out_s...  12.4 us
    unnamed x38, local copies, waits for them, and re-layouts  11.8 us
    all_to_all x3, waiting for transfers between devices, exchange(): return lax.all_to_all(value, axes, 0, 0)  10.3 us
    pallas_call x1, Pallas kernels, mean_kernel(): pl.pallas_call(body, out_shape=jax.ShapeDtypeStruct((columns, tests), bf1...  8.95 us
    ppermute x1, waiting for transfers between devices, shards(): lax.ppermute(train_rows, panel_axes, backward)  5.95 us
  transfers between devices with their start and end apart: 7, of which 6 were waited for; matrix products, arithmetic and copies ran while one was open for 0% of the time, Pallas kernels for 12%

profile of v1, /device:TPU:65, one launch (start us, length us, event | category | flops | bytes accessed | tf_op | source)
XLA Modules:
  0.0 190.0 jit_solution(16365747753846800840)
XLA Ops:
  0.0 1.3 copy-done
  1.3 0.9 copy-done.4
  2.2 2.3 %mixer.1 = f32[16,32,256]{2,1,0:T(8,128)} custom-call(bf16[320,2048]{1,0:T(8,128)(2,1)S(1)} %bitcast.11, f32[10,32,64]{2,1,0:T(8,128)S(1)} %bitcast.14), custom_call_target="tpu_custom_call" | custom-call | tf_op jit(solution)/shard_map/mixer/pallas_call | solution.py:49
  4.5 44.9 %all-to-all-start = ((f32[16,32,256]{2,1,0:T(8,128)}), f32[16,32,256]{2,1,0:T(8,128)S(1)}, u32[]{:S(2)}, u32[]{:S(2)}) async-start(f32[16,32,256]{2,1,0:T(8,128)} %mixer.1), calls=%async_computation | async-start | bytes 1048576 | tf_op jit(solution)/shard_map/all_to_all | solution.py:411
  49.5 0.7 copy-done.15
  50.2 0.7 copy-done.16
  50.9 0.2 points.1
  51.1 4.8 %collective-permute-start.1 = (bf16[16,2048]{1,0:T(8,128)(2,1)S(1)}, bf16[16,2048]{1,0:T(8,128)(2,1)S(1)}, u32[]{:S(2)}, u32[]{:S(2)}) collective-permute-start(bf16[16,2048]{1,0:T(8,128)(2,1)S(1)} %get-tuple-element.36.mine_ref), channel_id=1, source_target_pairs={{1,0},{2,1},{3,2},{4,3},{5,4},{6,5},{7,6},{8,7},{9,8},{10,9},{11,1... | collective-permute-start | bytes 196616 | tf_op jit(solution)/shard_map/ppermute | solution.py:475
  55.9 2.0 %collective-permute-start = (bf16[16,2048]{1,0:T(8,128)(2,1)S(1)}, bf16[16,2048]{1,0:T(8,128)(2,1)S(1)}, u32[]{:S(2)}, u32[]{:S(2)}) collective-permute-start(bf16[16,2048]{1,0:T(8,128)(2,1)S(1)} %get-tuple-element.36.mine_ref), channel_id=1, source_target_pairs={{0,1},{1,2},{2,3},{3,4},{4,5},{5,6},{6,7},{7,8},{8,9},{9,10},{10,1... | collective-permute-start | bytes 196616 | tf_op jit(solution)/shard_map/ppermute | solution.py:473
  57.8 0.7 broadcast_subtract_fusion
  58.5 0.1 slice_bitcast_fusion
  58.6 6.0 %collective-permute-done.1.after_ref = bf16[16,2048]{1,0:T(8,128)(2,1)S(1)} collective-permute-done((bf16[16,2048]{1,0:T(8,128)(2,1)S(1)}, bf16[16,2048]{1,0:T(8,128)(2,1)S(1)}, u32[]{:S(2)}, u32[]{:S(2)}) %collective-permute-start.1) | collective-permute-done | bytes 65568 | tf_op jit(solution)/shard_map/ppermute | solution.py:475
  64.5 0.8 collective-permute-done.before_ref
  65.3 1.3 copy-done.1
  66.6 1.6 copy-done.3
  68.2 0.9 copy-done.5
  69.1 0.9 copy-done.12
  70.1 0.7 copy-done.17
  70.8 5.1 %local.1 = (f32[64,2048]{1,0:T(8,128)S(1)}, f32[64,256]{1,0:T(8,128)S(1)}) custom-call(bf16[64,2048]{1,0:T(8,128)(2,1)S(1)} %copy-done.12, s32[1,2048]{1,0:T(1,128)S(1)} %copy-done.17, bf16[4,512,512]{2,1,0:T(8,128)(2,1)S(1)} %copy-done.3, bf16[320,2048]{1,0:T(8,128)(2,1)S(1)} %bitcast.12, f32[10,32,64]{2,1,0:T(8,128)S(1)} %bitcast.15), custom_call_target="tpu_custom_call" | custom-call | tf_op jit(solution)/shard_map/local/pallas_call | solution.py:49
  75.8 0.0 copy-start.8
  75.8 0.8 copy-done.8
  76.6 0.0 all-to-all-done.refs_1_
  76.7 0.7 broadcast_in_dim.4
  77.4 7.8 %all-to-all-start.1 = ((f32[16,32,128]{2,1,0:T(8,128)}), f32[16,32,128]{2,1,0:T(8,128)S(1)}, u32[]{:S(2)}, u32[]{:S(2)}) async-start(f32[16,32,128]{2,1,0:T(8,128)} %broadcast_in_dim.4), calls=%async_computation.1 | async-start | bytes 524288 | tf_op jit(solution)/shard_map/all_to_all | solution.py:411
  85.2 0.1 pad_add_fusion.refs_0_
  85.3 0.0 copy-done.13
  85.3 0.0 copy-done.10
  85.3 8.3 %near_early.1.refs_4_ = bf16[4,512,2048]{2,1,0:T(8,128)(2,1)} custom-call(s32[4]{0:T(128)S(1)} %get-tuple-element.34.slots_ref, bf16[16,2048]{1,0:T(8,128)(2,1)S(1)} %collective-permute-done.before_ref, bf16[16,2048]{1,0:T(8,128)(2,1)S(1)} %get-tuple-element.36.mine_ref, bf16[16,2048]{1,0:T(8,128)(2,1)S(1)} %collective-permute-done.1.after_ref, ...), custom_call_target="tpu_custom_call" | custom-call | tf_op jit(solution)/shard_map/near_early/pallas_call | solution.py:165
  93.6 6.9 %all-to-all-done.1.refs_2_ = f32[16,32,128]{2,1,0:T(8,128)S(1)} async-done(((f32[16,32,128]{2,1,0:T(8,128)}), f32[16,32,128]{2,1,0:T(8,128)S(1)}, u32[]{:S(2)}, u32[]{:S(2)}) %all-to-all-start.1) | async-done | bytes 262176 | tf_op jit(solution)/shard_map/all_to_all | solution.py:411
  100.6 1.6 operator.1
  102.2 8.5 %all-to-all-start.2 = ((bf16[16,48,256]{2,1,0:T(8,128)(2,1)}), bf16[16,48,256]{2,1,0:T(8,128)(2,1)S(1)}, u32[]{:S(2)}, u32[]{:S(2)}) async-start(bf16[16,48,256]{2,1,0:T(8,128)(2,1)} %operator.1), calls=%async_computation.2 | async-start | bytes 786432 | tf_op jit(solution)/shard_map/all_to_all | solution.py:411
  110.7 0.8 copy-done.11
  111.6 8.3 %near_late.1.refs_5_ = bf16[4,512,2048]{2,1,0:T(8,128)(2,1)} custom-call(s32[4]{0:T(128)S(1)} %get-tuple-element.41.slots_ref, bf16[16,2048]{1,0:T(8,128)(2,1)S(1)} %copy-done.11, bf16[16,2048]{1,0:T(8,128)(2,1)S(1)} %get-tuple-element.36.mine_ref, bf16[16,2048]{1,0:T(8,128)(2,1)S(1)} %collective-permute-done.1.after_ref, ...), custom_call_target="tpu_custom_call" | custom-call | tf_op jit(solution)/shard_map/near_late/pallas_call | solution.py:165
  119.9 3.3 %all-to-all-done.2.refs_1_ = bf16[16,48,256]{2,1,0:T(8,128)(2,1)S(1)} async-done(((bf16[16,48,256]{2,1,0:T(8,128)(2,1)}), bf16[16,48,256]{2,1,0:T(8,128)(2,1)S(1)}, u32[]{:S(2)}, u32[]{:S(2)}) %all-to-all-start.2) | async-done | bytes 393248 | tf_op jit(solution)/shard_map/all_to_all | solution.py:411
  123.2 1.1 eliminate.1
  124.3 11.9 %all_to_all.30.refs_1_ = f32[16,4,256]{2,1,0:T(4,128)S(1)} all-to-all(f32[16,4,256]{2,1,0:T(4,128)S(1)} %eliminate.1), channel_id=1, replica_groups=mesh['grp'=2,'z'=16,'core'=2,'sub'=8] {'core','sub'}, dimensions={0} | all-to-all | bytes 131072 | tf_op jit(solution)/shard_map/all_to_all | solution.py:411
  136.2 16.9 %all_to_all.31.refs_2_ = f32[16,4,128]{2,1,0:T(4,128)S(1)} all-to-all(f32[16,4,128]{2,1,0:T(4,128)S(1)} %broadcast_in_dim.5), channel_id=1, replica_groups=mesh['grp'=2,'z'=16,'core'=2,'sub'=8] {'z'}, dimensions={0} | all-to-all | bytes 65536 | tf_op jit(solution)/shard_map/all_to_all | solution.py:411
  153.0 0.6 subtree.1
  153.6 12.2 %all_to_all.32.refs_0_ = f32[16,8,256]{2,1,0:T(8,128)S(1)} all-to-all(f32[16,8,256]{2,1,0:T(8,128)S(1)} %subtree.1), channel_id=1, replica_groups=mesh['grp'=2,'z'=16,'core'=2,'sub'=8] {'core','sub'}, dimensions={0} | all-to-all | bytes 262144 | tf_op jit(solution)/shard_map/all_to_all | solution.py:411
  165.8 0.0 copy-done.2
  165.8 1.0 copy-done.9
  166.8 0.8 weights.1
  167.7 4.4 %collective-permute-start.3 = (bf16[64,2048]{1,0:T(8,128)(2,1)S(1)}, bf16[64,2048]{1,0:T(8,128)(2,1)S(1)}, u32[]{:S(2)}, u32[]{:S(2)}) collective-permute-start(bf16[64,2048]{1,0:T(8,128)(2,1)S(1)} %get-tuple-element.45.refs_2_), channel_id=1, source_target_pairs={{1,0},{2,1},{3,2},{4,3},{5,4},{6,5},{7,6},{8,7},{9,8},{10,9},{11,1... | collective-permute-start | bytes 786440 | tf_op jit(solution)/shard_map/ppermute | solution.py:536
  172.1 2.0 %collective-permute-start.2 = (bf16[64,2048]{1,0:T(8,128)(2,1)S(1)}, bf16[64,2048]{1,0:T(8,128)(2,1)S(1)}, u32[]{:S(2)}, u32[]{:S(2)}) collective-permute-start(bf16[64,2048]{1,0:T(8,128)(2,1)S(1)} %get-tuple-element.45.refs_2_), channel_id=1, source_target_pairs={{0,1},{1,2},{2,3},{3,4},{4,5},{5,6},{6,7},{7,8},{8,9},{9,10},{10,1... | collective-permute-start | bytes 786440 | tf_op jit(solution)/shard_map/ppermute | solution.py:535
  174.1 0.8 far.1.refs_6_
  174.9 3.3 %collective-permute-done.3.refs_3_ = bf16[64,2048]{1,0:T(8,128)(2,1)S(1)} collective-permute-done((bf16[64,2048]{1,0:T(8,128)(2,1)S(1)}, bf16[64,2048]{1,0:T(8,128)(2,1)S(1)}, u32[]{:S(2)}, u32[]{:S(2)}) %collective-permute-start.3) | collective-permute-done | bytes 262176 | tf_op jit(solution)/shard_map/ppermute | solution.py:536
  178.2 2.8 %collective-permute-done.2.refs_1_ = bf16[64,2048]{1,0:T(8,128)(2,1)S(1)} collective-permute-done((bf16[64,2048]{1,0:T(8,128)(2,1)S(1)}, bf16[64,2048]{1,0:T(8,128)(2,1)S(1)}, u32[]{:S(2)}, u32[]{:S(2)}) %collective-permute-start.2) | collective-permute-done | bytes 262176 | tf_op jit(solution)/shard_map/ppermute | solution.py:535
  181.0 9.0 %posterior_mean.1 = bf16[64,2048]{1,0:T(8,128)(2,1)} custom-call(s32[8]{0:T(128)S(1)} %fusion.refs_0_, bf16[64,2048]{1,0:T(8,128)(2,1)S(1)} %collective-permute-done.2.refs_1_, bf16[64,2048]{1,0:T(8,128)(2,1)S(1)} %get-tuple-element.45.refs_2_, bf16[64,2048]{1,0:T(8,128)(2,1)S(1)} %collective-permute-done.3.refs_3_, ...), custom_call_target="tpu_custom_call" | custom-call | tf_op jit(solution)/shard_map/posterior_mean/pallas_call | solution.py:390
  (28 shorter events, 0.1 us)
Async XLA Ops:
  0.0 1.3 copy-start
  1.3 0.9 copy-start.4
  4.5 72.1 %all-to-all-start = ((f32[16,32,256]{2,1,0:T(8,128)}), f32[16,32,256]{2,1,0:T(8,128)S(1)}, u32[]{:S(2)}, u32[]{:S(2)}) async-start(f32[16,32,256]{2,1,0:T(8,128)} %mixer.1), calls=%async_computation | async-start | bytes 1048576 | tf_op jit(solution)/shard_map/all_to_all | solution.py:411
  49.5 0.7 copy-start.15
  50.2 0.7 copy-start.16
  51.1 13.4 %collective-permute-start.1 = (bf16[16,2048]{1,0:T(8,128)(2,1)S(1)}, bf16[16,2048]{1,0:T(8,128)(2,1)S(1)}, u32[]{:S(2)}, u32[]{:S(2)}) collective-permute-start(bf16[16,2048]{1,0:T(8,128)(2,1)S(1)} %get-tuple-element.36.mine_ref), channel_id=1, source_target_pairs={{1,0},{2,1},{3,2},{4,3},{5,4},{6,5},{7,6},{8,7},{9,8},{10,9},{11,1... | collective-permute-start | bytes 196616 | tf_op jit(solution)/shard_map/ppermute | solution.py:475
  55.9 9.4 %collective-permute-start = (bf16[16,2048]{1,0:T(8,128)(2,1)S(1)}, bf16[16,2048]{1,0:T(8,128)(2,1)S(1)}, u32[]{:S(2)}, u32[]{:S(2)}) collective-permute-start(bf16[16,2048]{1,0:T(8,128)(2,1)S(1)} %get-tuple-element.36.mine_ref), channel_id=1, source_target_pairs={{0,1},{1,2},{2,3},{3,4},{4,5},{5,6},{6,7},{7,8},{8,9},{9,10},{10,1... | collective-permute-start | bytes 196616 | tf_op jit(solution)/shard_map/ppermute | solution.py:473
  65.3 1.3 copy-start.1
  66.6 1.6 copy-start.3
  68.2 0.9 copy-start.5
  69.1 0.9 copy-start.12
  70.1 0.7 copy-start.17
  70.8 14.5 %copy-start.10 = (bf16[16,2048]{1,0:T(8,128)(2,1)}, bf16[16,2048]{1,0:T(8,128)(2,1)S(1)}, u32[]{:S(2)}) copy-start(bf16[16,2048]{1,0:T(8,128)(2,1)S(1)} %collective-permute-done.before_ref) | copy-start | bytes 196612
  75.8 0.8 copy-start.8
  76.6 8.7 %copy-start.13 = (f32[64,256]{1,0:T(8,128)}, f32[64,256]{1,0:T(8,128)S(1)}, u32[]{:S(2)}) copy-start(f32[64,256]{1,0:T(8,128)S(1)} %get-tuple-element.32.refs_0_) | copy-start | bytes 196612
  77.4 23.2 %all-to-all-start.1 = ((f32[16,32,128]{2,1,0:T(8,128)}), f32[16,32,128]{2,1,0:T(8,128)S(1)}, u32[]{:S(2)}, u32[]{:S(2)}) async-start(f32[16,32,128]{2,1,0:T(8,128)} %broadcast_in_dim.4), calls=%async_computation.1 | async-start | bytes 524288 | tf_op jit(solution)/shard_map/all_to_all | solution.py:411
  85.3 80.5 %copy-start.2 = (bf16[10,32,2048]{2,1,0:T(8,128)(2,1)S(1)}, bf16[10,32,2048]{2,1,0:T(8,128)(2,1)}, u32[]{:S(2)}) copy-start(bf16[10,32,2048]{2,1,0:T(8,128)(2,1)} %param.12) | copy-start | bytes 3932164
  85.3 80.5 %copy-start.6 = (f32[1,10,32,64]{3,2,1,0:T(8,128)S(1)}, f32[1,10,32,64]{3,2,1,0:T(8,128)}, u32[]{:S(2)}) copy-start(f32[1,10,32,64]{3,2,1,0:T(8,128)} %param.13) | copy-start | bytes 245764
  93.6 80.4 %copy-start.18 = (s32[1,8]{1,0:T(1,128)S(1)}, s32[1,8]{1,0:T(1,128)}, u32[]{:S(2)}) copy-start(s32[1,8]{1,0:T(1,128)} %param.17) | copy-start | bytes 100
  93.6 80.4 %copy-start.7 = (bf16[8,32,2048]{2,1,0:T(8,128)(2,1)S(1)}, bf16[8,32,2048]{2,1,0:T(8,128)(2,1)}, u32[]{:S(2)}) copy-start(bf16[8,32,2048]{2,1,0:T(8,128)(2,1)} %param.16) | copy-start | bytes 3145732
  102.2 21.0 %copy-start.14 = (f32[64,256]{1,0:T(8,128)S(1)}, f32[64,256]{1,0:T(8,128)}, u32[]{:S(2)}) copy-start(f32[64,256]{1,0:T(8,128)} %copy-done.13) | copy-start | bytes 196612
  102.2 21.0 %all-to-all-start.2 = ((bf16[16,48,256]{2,1,0:T(8,128)(2,1)}), bf16[16,48,256]{2,1,0:T(8,128)(2,1)S(1)}, u32[]{:S(2)}, u32[]{:S(2)}) async-start(bf16[16,48,256]{2,1,0:T(8,128)(2,1)} %operator.1), calls=%async_computation.2 | async-start | bytes 786432 | tf_op jit(solution)/shard_map/all_to_all | solution.py:411
  110.7 0.8 copy-start.11
  165.8 1.0 copy-start.9
  167.7 10.5 %collective-permute-start.3 = (bf16[64,2048]{1,0:T(8,128)(2,1)S(1)}, bf16[64,2048]{1,0:T(8,128)(2,1)S(1)}, u32[]{:S(2)}, u32[]{:S(2)}) collective-permute-start(bf16[64,2048]{1,0:T(8,128)(2,1)S(1)} %get-tuple-element.45.refs_2_), channel_id=1, source_target_pairs={{1,0},{2,1},{3,2},{4,3},{5,4},{6,5},{7,6},{8,7},{9,8},{10,9},{11,1... | collective-permute-start | bytes 786440 | tf_op jit(solution)/shard_map/ppermute | solution.py:536
  172.1 8.9 %collective-permute-start.2 = (bf16[64,2048]{1,0:T(8,128)(2,1)S(1)}, bf16[64,2048]{1,0:T(8,128)(2,1)S(1)}, u32[]{:S(2)}, u32[]{:S(2)}) collective-permute-start(bf16[64,2048]{1,0:T(8,128)(2,1)S(1)} %get-tuple-element.45.refs_2_), channel_id=1, source_target_pairs={{0,1},{1,2},{2,3},{3,4},{4,5},{5,6},{6,7},{7,8},{8,9},{9,10},{10,1... | collective-permute-start | bytes 786440 | tf_op jit(solution)/shard_map/ppermute | solution.py:535

commit v2 on v1

--- a/solution.py
+++ b/solution.py
@@ -38,7 +38,7 @@
     return lax.dot_general(left, right, dims, precision=highest, preferred_element_type=f32)
 
 
-def whole_call(body, out_shape, name, scalars=0, scratch=()):
+def whole_call(body, out_shape, name, scalars=0, scratch=(), limit=20 << 20):
     def call(*operands):
         specs = [
             pl.BlockSpec(memory_space=pltpu.SMEM if i < scalars else pltpu.VMEM)
@@ -53,7 +53,7 @@
             out_specs=out_specs if single else [out_specs] * len(out_shape),
             scratch_shapes=list(scratch),
             name=name,
-            compiler_params=pltpu.CompilerParams(vmem_limit_bytes=20 << 20),
+            compiler_params=pltpu.CompilerParams(vmem_limit_bytes=limit),
         )(*operands)
 
     return call
@@ -159,12 +159,12 @@
         out_ref[0, :, start : start + step] = ((1.0 + scaled) * jnp.exp(-scaled)).astype(bf16)
 
 
-def distance_kernel(slots, sides, test_features, leaf_size, name):
+def distance_kernel(slots, sides, test_features, leaf_size, name, store=pltpu.HBM):
     tests = test_features.shape[1]
     operands = (*sides, test_features)
     return pl.pallas_call(
         distance_body,
-        out_shape=pltpu.HBM((slots.shape[0], leaf_size, tests), bf16),
+        out_shape=store((slots.shape[0], leaf_size, tests), bf16),
         grid_spec=pltpu.PrefetchScalarGridSpec(
             num_scalar_prefetch=1,
             grid=(slots.shape[0],),
@@ -344,7 +344,7 @@
 
 
 def mean_body(
-    slots_ref, before_ref, mine_ref, after_ref, early_ref, late_ref, far_ref,
+    slots_ref, before_ref, mine_ref, after_ref, early_ref, late_ref, last_ref, far_ref,
     out_ref, window_ref, near_ref, *, leaf_size, factor,
 ):
     step = pl.program_id(0)
@@ -361,20 +361,24 @@
                 ]
         near_ref[...] = far_ref[...]
 
-    near_ref[...] += jnp.dot(
-        window_ref[slots_ref[step]], early_ref[0], preferred_element_type=f32
-    ) + jnp.dot(window_ref[slots_ref[steps + step]], late_ref[0], preferred_element_type=f32)
+    def part_of(slot, ref):
+        return jnp.dot(window_ref[slots_ref[slot]], ref[0], preferred_element_type=f32)
+
+    @pl.when(step < steps - 1)
+    def _():
+        near_ref[...] += part_of(step, early_ref) + part_of(steps + step, late_ref)
 
     @pl.when(step == steps - 1)
     def _():
-        out_ref[...] = (near_ref[...] * factor).astype(bf16)
+        near = near_ref[...] + part_of(step, early_ref) + part_of(steps + step, last_ref)
+        out_ref[...] = (near * factor).astype(bf16)
 
 
 def in_hbm(value):
     return pltpu.with_memory_space_constraint(value, pltpu.HBM)
 
 
-def mean_kernel(slots, before, mine, after, early, late, far, factor):
+def mean_kernel(slots, before, mine, after, early, late, last, far, factor):
     steps, leaf_size, tests = early.shape
     columns, points = mine.shape
     whole = [before, mine, after]
@@ -382,7 +386,13 @@
     def fixed(array):
         return pl.BlockSpec(array.shape, lambda i, s: (0,) * array.ndim)
 
-    moving = pl.BlockSpec((1, leaf_size, tests), lambda i, s: (i, 0, 0))
+    block = (1, leaf_size, tests)
+    final = late.shape[0] - 1
+    moving = [
+        pl.BlockSpec(block, lambda i, s: (i, 0, 0)),
+        pl.BlockSpec(block, lambda i, s: (jnp.minimum(i, final), 0, 0)),
+        pl.BlockSpec(memory_space=pltpu.VMEM),
+    ]
 
     def body(*refs):
         mean_body(*refs, leaf_size=leaf_size, factor=factor)
@@ -394,7 +404,7 @@
             num_scalar_prefetch=1,
             grid=(steps,),
             in_specs=[fixed(a) for a in whole]
-            + [moving, moving]
+            + moving
             + [fixed(far)],
             out_specs=pl.BlockSpec((columns, tests), lambda i, s: (0, 0)),
             scratch_shapes=[
@@ -404,7 +414,7 @@
         ),
         compiler_params=pltpu.CompilerParams(vmem_limit_bytes=24 << 20),
         name="posterior_mean",
-    )(slots, *whole, in_hbm(early), in_hbm(late), far)
+    )(slots, *whole, in_hbm(early), in_hbm(late), last, far)
 
 
 def exchange(value, axes):
@@ -455,7 +465,7 @@
         mixer_body(*refs, local_levels=local_levels, part=part)
 
     effect = whole_call(
-        mixer, jax.ShapeDtypeStruct((low_count, 2 * part, width), f32), "mixer"
+        mixer, jax.ShapeDtypeStruct((low_count, 2 * part, width), f32), "mixer", limit=None
     )(basis, mixers)
     effect, train_coords = tie(effect, train_coords)
     spread = exchange(effect, low_axes)
@@ -469,12 +479,7 @@
     )(train_coords, test_coords)
     forward = [(i, i + 1) for i in range(panels - 1)]
     backward = [(i + 1, i) for i in range(panels - 1)]
-    sides = (
-        lax.ppermute(train_rows, panel_axes, forward),
-        train_rows,
-        lax.ppermute(train_rows, panel_axes, backward),
-    )
-    *sides, tree_order = tie(*sides, tree_order)
+    train_rows, tree_order = tie(train_rows, tree_order)
 
     state, terms = whole_call(
         local_body,
@@ -483,12 +488,18 @@
             jax.ShapeDtypeStruct((columns, width), f32),
         ],
         "local",
+        limit=None,
     )(targets, tree_order, leaf_inverse, basis, mixers)
     terms, spread = tie(terms, spread)
 
     slots = near_leaves[0] - (position - 1) * leaf_count
     total = jnp.sum(spread, axis=0)[:, low_width:]
-    early_slots, total = tie(slots[:half_slots], total)
+    early_slots, train_rows, total = tie(slots[:half_slots], train_rows, total)
+    sides = (
+        lax.ppermute(train_rows, panel_axes, forward),
+        train_rows,
+        lax.ppermute(train_rows, panel_axes, backward),
+    )
     high_spread = gathered(total, "z")
     early = distance_kernel(early_slots, sides, test_rows, leaf_size, "near_early")
     early, high_spread = tie(early, high_spread)
@@ -499,7 +510,7 @@
     operators = whole_call(
         operator, jax.ShapeDtypeStruct((low_count, 3 * part, width), bf16), "operator", 1
     )(place, spread, high_spread)
-    late_slots, operators = tie(slots[half_slots:], operators)
+    late_slots, operators = tie(slots[half_slots:-1], operators)
     operators = exchange(operators, low_axes)
     late = distance_kernel(late_slots, sides, test_rows, leaf_size, "near_late")
     late, operators = tie(late, operators)
@@ -532,6 +543,10 @@
         ],
         "weights",
     )(sums, state, basis, mixers)
+    last_slot, weights = tie(slots[-1:], weights)
+    last = distance_kernel(
+        last_slot, sides, test_rows, leaf_size, "near_last", jax.ShapeDtypeStruct
+    )
     before = lax.ppermute(weights, panel_axes, forward)
     after = lax.ppermute(weights, panel_axes, backward)
     factor = 2.0 / math.sqrt(near_leaves.shape[1] * leaf_size)
@@ -542,7 +557,7 @@
     far = whole_call(distant, jax.ShapeDtypeStruct((columns, points), f32), "far")(
         joined, operators, test_basis.reshape(width, -1)
     )
-    return mean_kernel(slots, before, weights, after, early, late, far, factor)
+    return mean_kernel(slots, before, weights, after, early, late, last, far, factor)
 
 
 def solution(mesh):

time: 191 us -> 188 us (0.984)
  local copies, waits for them, and re-layouts: 12.7 us -> 2.55 us
  starting transfers between devices: 74.4 us -> 80.5 us
  Pallas kernels: 38 us -> 42.8 us
  blocking collectives: 40.9 us -> 36.8 us
    unnamed x38 -> x16, local copies, waits for them, and re-layouts: 11.8 us -> 1.07 us
    all_to_all x3 -> x4, waiting for transfers between devices: 10.3 us -> 19.1 us  [exchange(): return lax.all_to_all(value, axes, 0, 0)]
    all_to_all x3 -> x4, starting transfers between devices: 61.3 us -> 66.8 us  [exchange(): return lax.all_to_all(value, axes, 0, 0)]
    pallas_call x8, Pallas kernels: 12.4 us -> 17.1 us  [call(): pl.pallas_call(body, out_shape=out_shape, in_specs=specs, out_specs=out_s...]
    ppermute x1, waiting for transfers between devices: 5.95 us -> 1.67 us  [shards(): lax.ppermute(train_rows, panel_axes, backward)]
    all_to_all x3 -> x2, blocking collectives: 40.9 us -> 36.8 us  [exchange(): return lax.all_to_all(value, axes, 0, 0)]
    ppermute x1, waiting for transfers between devices: 2.83 us -> 0.01 us  [shards(): before = lax.ppermute(weights, panel_axes, forward)]
    pallas_call x2 -> x3, Pallas kernels: 16.6 us -> 17.2 us  [distance_kernel(): pl.pallas_call(distance_body, out_shape=store((slots.shape[0], leaf_size,...]
  transfers between devices with their start and end apart: 7 -> 8, of which waited for: 6 -> 6; matrix products, arithmetic and copies ran while one was open for 0% -> 0% of each run, Pallas kernels for 12% -> 14%
where the time goes in v2:
time: 188 us; the launch traced here: 187 us
  starting transfers between devices  80.5 us (43%)
  Pallas kernels  42.8 us (23%)
  blocking collectives  36.8 us (20%)
  waiting for transfers between devices  24 us (13%)
  local copies, waits for them, and re-layouts  2.55 us (1%)
    all_to_all x4, starting transfers between devices, exchange(): return lax.all_to_all(value, axes, 0, 0)  66.8 us
    all_to_all x2, blocking collectives, exchange(): return lax.all_to_all(value, axes, 0, 0)  36.8 us
    all_to_all x4, waiting for transfers between devices, exchange(): return lax.all_to_all(value, axes, 0, 0)  19.1 us
    pallas_call x3, Pallas kernels, distance_kernel(): pl.pallas_call(distance_body, out_shape=store((slots.shape[0], leaf_size,...  17.2 us
    pallas_call x8, Pallas kernels, call(): pl.pallas_call(body, out_shape=out_shape, in_specs=specs, out_specs=out_s...  17.1 us
    pallas_call x1, Pallas kernels, mean_kernel(): pl.pallas_call(body, out_shape=jax.ShapeDtypeStruct((columns, tests), bf1...  8.46 us
  transfers between devices with their start and end apart: 8, of which 6 were waited for; matrix products, arithmetic and copies ran while one was open for 0% of the time, Pallas kernels for 14%

profile of v2, /device:TPU:65, one launch (start us, length us, event | category | flops | bytes accessed | tf_op | source)
XLA Modules:
  0.0 186.9 jit_solution(9325013786467089429)
XLA Ops:
  0.0 0.0 copy-start.5
  0.0 0.0 copy-start.6
  0.0 3.6 %mixer.1 = f32[16,32,256]{2,1,0:T(8,128)} custom-call(bf16[320,2048]{1,0:T(8,128)(2,1)} %bitcast.12, f32[10,32,64]{2,1,0:T(8,128)} %bitcast.15), custom_call_target="tpu_custom_call" | custom-call | tf_op jit(solution)/shard_map/mixer/pallas_call | solution.py:49
  3.6 44.9 %all-to-all-start = ((f32[16,32,256]{2,1,0:T(8,128)}), f32[16,32,256]{2,1,0:T(8,128)S(1)}, u32[]{:S(2)}, u32[]{:S(2)}) async-start(f32[16,32,256]{2,1,0:T(8,128)} %mixer.1), calls=%async_computation | async-start | bytes 1048576 | tf_op jit(solution)/shard_map/all_to_all | solution.py:421
  48.6 0.0 copy-start.7
  48.6 0.0 copy-done.5
  48.6 0.0 copy-done.6
  48.6 0.2 points.1
  48.8 7.8 %local.1 = (f32[64,2048]{1,0:T(8,128)}, f32[64,256]{1,0:T(8,128)}) custom-call(bf16[64,2048]{1,0:T(8,128)(2,1)} %targets_ref.1, s32[1,2048]{1,0:T(1,128)} %order_ref, bf16[4,512,512]{2,1,0:T(8,128)(2,1)} %inverse_ref.1, bf16[320,2048]{1,0:T(8,128)(2,1)} %bitcast.13, f32[10,32,64]{2,1,0:T(8,128)} %bitcast.16), custom_call_target="tpu_custom_call" | custom-call | tf_op jit(solution)/shard_map/local/pallas_call | solution.py:49
  56.6 0.0 copy-done.7
  56.6 6.8 %all-to-all-done.refs_1_ = f32[16,32,256]{2,1,0:T(8,128)S(1)} async-done(((f32[16,32,256]{2,1,0:T(8,128)}), f32[16,32,256]{2,1,0:T(8,128)S(1)}, u32[]{:S(2)}, u32[]{:S(2)}) %all-to-all-start) | async-done | bytes 524320 | tf_op jit(solution)/shard_map/all_to_all | solution.py:421
  63.4 0.7 broadcast_in_dim.4
  64.1 7.2 %all-to-all-start.1 = ((f32[16,32,128]{2,1,0:T(8,128)}), f32[16,32,128]{2,1,0:T(8,128)S(1)}, u32[]{:S(2)}, u32[]{:S(2)}) async-start(f32[16,32,128]{2,1,0:T(8,128)} %broadcast_in_dim.4), calls=%async_computation.1 | async-start | bytes 524288 | tf_op jit(solution)/shard_map/all_to_all | solution.py:421
  71.3 0.1 slice_bitcast_fusion.1.slots_ref
  71.4 3.4 %collective-permute-start = (bf16[16,2048]{1,0:T(8,128)(2,1)S(1)}, bf16[16,2048]{1,0:T(8,128)(2,1)S(1)}, u32[]{:S(2)}, u32[]{:S(2)}) collective-permute-start(bf16[16,2048]{1,0:T(8,128)(2,1)S(1)} %get-tuple-element.37.mine_ref), channel_id=1, source_target_pairs={{0,1},{1,2},{2,3},{3,4},{4,5},{5,6},{6,7},{7,8},{8,9},{9,10},{10,1... | collective-permute-start | bytes 196616 | tf_op jit(solution)/shard_map/ppermute | solution.py:499
  74.9 3.4 %collective-permute-start.1 = (bf16[16,2048]{1,0:T(8,128)(2,1)S(1)}, bf16[16,2048]{1,0:T(8,128)(2,1)S(1)}, u32[]{:S(2)}, u32[]{:S(2)}) collective-permute-start(bf16[16,2048]{1,0:T(8,128)(2,1)S(1)} %get-tuple-element.37.mine_ref), channel_id=1, source_target_pairs={{1,0},{2,1},{3,2},{4,3},{5,4},{6,5},{7,6},{8,7},{9,8},{10,9},{11,1... | collective-permute-start | bytes 196616 | tf_op jit(solution)/shard_map/ppermute | solution.py:501
  78.3 0.1 pad_add_fusion.refs_0_
  78.3 0.2 collective-permute-done.before_ref
  78.5 1.7 collective-permute-done.1.after_ref
  80.2 8.3 %near_early.1.refs_4_ = bf16[4,512,2048]{2,1,0:T(8,128)(2,1)} custom-call(s32[4]{0:T(128)S(1)} %slice_bitcast_fusion.slots_ref, bf16[16,2048]{1,0:T(8,128)(2,1)S(1)} %collective-permute-done.before_ref, bf16[16,2048]{1,0:T(8,128)(2,1)S(1)} %get-tuple-element.37.mine_ref, bf16[16,2048]{1,0:T(8,128)(2,1)S(1)} %collective-permute-done.1.after_ref, ...), custom_call_target="tpu_custom_call" | custom-call | tf_op jit(solution)/shard_map/near_early/pallas_call | solution.py:165
  88.5 0.0 all-to-all-done.1.refs_2_
  88.5 1.6 operator.1
  90.1 8.9 %all-to-all-start.2 = ((bf16[16,48,256]{2,1,0:T(8,128)(2,1)}), bf16[16,48,256]{2,1,0:T(8,128)(2,1)S(1)}, u32[]{:S(2)}, u32[]{:S(2)}) async-start(bf16[16,48,256]{2,1,0:T(8,128)(2,1)} %operator.1), calls=%async_computation.2 | async-start | bytes 786432 | tf_op jit(solution)/shard_map/all_to_all | solution.py:421
  99.0 0.0 copy-start.4
  99.0 0.0 copy-start.1
  99.0 6.7 %near_late.1.refs_5_ = bf16[3,512,2048]{2,1,0:T(8,128)(2,1)} custom-call(s32[3]{0:T(128)S(1)} %slice_bitcast_fusion.1.slots_ref, bf16[16,2048]{1,0:T(8,128)(2,1)S(1)} %collective-permute-done.before_ref, bf16[16,2048]{1,0:T(8,128)(2,1)S(1)} %get-tuple-element.37.mine_ref, bf16[16,2048]{1,0:T(8,128)(2,1)S(1)} %collective-permute-done.1.after_ref, ...), custom_call_target="tpu_custom_call" | custom-call | tf_op jit(solution)/shard_map/near_late/pallas_call | solution.py:165
  105.7 0.0 copy-start
  105.7 5.7 %all-to-all-done.2.refs_1_ = bf16[16,48,256]{2,1,0:T(8,128)(2,1)S(1)} async-done(((bf16[16,48,256]{2,1,0:T(8,128)(2,1)}), bf16[16,48,256]{2,1,0:T(8,128)(2,1)S(1)}, u32[]{:S(2)}, u32[]{:S(2)}) %all-to-all-start.2) | async-done | bytes 393248 | tf_op jit(solution)/shard_map/all_to_all | solution.py:421
  111.5 0.0 copy-done.4
  111.5 1.1 eliminate.1
  112.6 11.9 %all_to_all.30.refs_1_ = f32[16,4,256]{2,1,0:T(4,128)S(1)} all-to-all(f32[16,4,256]{2,1,0:T(4,128)S(1)} %eliminate.1), channel_id=1, replica_groups=mesh['grp'=2,'z'=16,'core'=2,'sub'=8] {'core','sub'}, dimensions={0} | all-to-all | bytes 131072 | tf_op jit(solution)/shard_map/all_to_all | solution.py:421
  124.4 24.9 %all_to_all.31.refs_2_ = f32[16,4,128]{2,1,0:T(4,128)S(1)} all-to-all(f32[16,4,128]{2,1,0:T(4,128)S(1)} %broadcast_in_dim.5), channel_id=1, replica_groups=mesh['grp'=2,'z'=16,'core'=2,'sub'=8] {'z'}, dimensions={0} | all-to-all | bytes 65536 | tf_op jit(solution)/shard_map/all_to_all | solution.py:421
  149.4 1.2 subtree.1
  150.6 5.8 %all-to-all-start.5 = ((f32[16,8,256]{2,1,0:T(8,128)}), f32[16,8,256]{2,1,0:T(8,128)S(1)}, u32[]{:S(2)}, u32[]{:S(2)}) async-start(f32[16,8,256]{2,1,0:T(8,128)} %subtree.1), calls=%async_computation.5 | async-start | bytes 262144 | tf_op jit(solution)/shard_map/all_to_all | solution.py:421
  156.4 0.7 slice.24
  157.0 6.5 %all-to-all-done.5.refs_0_ = f32[16,8,256]{2,1,0:T(8,128)S(1)} async-done(((f32[16,8,256]{2,1,0:T(8,128)}), f32[16,8,256]{2,1,0:T(8,128)S(1)}, u32[]{:S(2)}, u32[]{:S(2)}) %all-to-all-start.5) | async-done | bytes 131104 | tf_op jit(solution)/shard_map/all_to_all | solution.py:421
  163.6 0.0 copy-done.1
  163.6 0.0 copy-done
  163.6 1.0 copy-done.3
  164.6 0.8 weights.1
  165.4 3.6 %collective-permute-start.2 = (bf16[64,2048]{1,0:T(8,128)(2,1)S(1)}, bf16[64,2048]{1,0:T(8,128)(2,1)S(1)}, u32[]{:S(2)}, u32[]{:S(2)}) collective-permute-start(bf16[64,2048]{1,0:T(8,128)(2,1)S(1)} %get-tuple-element.46.refs_2_), channel_id=1, source_target_pairs={{0,1},{1,2},{2,3},{3,4},{4,5},{5,6},{6,7},{7,8},{8,9},{9,10},{10,1... | collective-permute-start | bytes 786440 | tf_op jit(solution)/shard_map/ppermute | solution.py:550
  169.1 3.2 %collective-permute-start.3 = (bf16[64,2048]{1,0:T(8,128)(2,1)S(1)}, bf16[64,2048]{1,0:T(8,128)(2,1)S(1)}, u32[]{:S(2)}, u32[]{:S(2)}) collective-permute-start(bf16[64,2048]{1,0:T(8,128)(2,1)S(1)} %get-tuple-element.46.refs_2_), channel_id=1, source_target_pairs={{1,0},{2,1},{3,2},{4,3},{5,4},{6,5},{7,6},{8,7},{9,8},{10,9},{11,1... | collective-permute-start | bytes 786440 | tf_op jit(solution)/shard_map/ppermute | solution.py:551
  172.3 0.0 copy-done.2
  172.3 0.8 far.1.refs_7_
  173.1 2.2 %near_last.1.refs_6_ = bf16[1,512,2048]{2,1,0:T(8,128)(2,1)S(1)} custom-call(s32[1]{0:T(128)} %bitcast.1.slots_ref, bf16[16,2048]{1,0:T(8,128)(2,1)S(1)} %collective-permute-done.before_ref, bf16[16,2048]{1,0:T(8,128)(2,1)S(1)} %get-tuple-element.37.mine_ref, bf16[16,2048]{1,0:T(8,128)(2,1)S(1)} %collective-permute-done.1.after_ref, ...), custom_call_target="tpu_custom_call" | custom-call | tf_op jit(solution)/shard_map/near_last/pallas_call | solution.py:165
  175.4 0.0 collective-permute-done.2.refs_1_
  175.4 3.0 %collective-permute-done.3.refs_3_ = bf16[64,2048]{1,0:T(8,128)(2,1)S(1)} collective-permute-done((bf16[64,2048]{1,0:T(8,128)(2,1)S(1)}, bf16[64,2048]{1,0:T(8,128)(2,1)S(1)}, u32[]{:S(2)}, u32[]{:S(2)}) %collective-permute-start.3) | collective-permute-done | bytes 262176 | tf_op jit(solution)/shard_map/ppermute | solution.py:551
  178.4 8.5 %posterior_mean.1 = bf16[64,2048]{1,0:T(8,128)(2,1)} custom-call(s32[8]{0:T(128)S(1)} %fusion.refs_0_, bf16[64,2048]{1,0:T(8,128)(2,1)S(1)} %collective-permute-done.2.refs_1_, bf16[64,2048]{1,0:T(8,128)(2,1)S(1)} %get-tuple-element.46.refs_2_, bf16[64,2048]{1,0:T(8,128)(2,1)S(1)} %collective-permute-done.3.refs_3_, ...), custom_call_target="tpu_custom_call" | custom-call | tf_op jit(solution)/shard_map/posterior_mean/pallas_call | solution.py:400
  (10 shorter events, 0.1 us)
Async XLA Ops:
  0.0 48.6 %copy-start.5 = (bf16[3,2048]{1,0:T(4,128)(2,1)S(1)}, bf16[3,2048]{1,0:T(4,128)(2,1)}, u32[]{:S(2)}) copy-start(bf16[3,2048]{1,0:T(4,128)(2,1)} %refs_0_) | copy-start | bytes 36868
  0.0 48.6 %copy-start.6 = (bf16[3,2048]{1,0:T(4,128)(2,1)S(1)}, bf16[3,2048]{1,0:T(4,128)(2,1)}, u32[]{:S(2)}) copy-start(bf16[3,2048]{1,0:T(4,128)(2,1)} %refs_1_.1) | copy-start | bytes 36868
  3.6 59.7 %all-to-all-start = ((f32[16,32,256]{2,1,0:T(8,128)}), f32[16,32,256]{2,1,0:T(8,128)S(1)}, u32[]{:S(2)}, u32[]{:S(2)}) async-start(f32[16,32,256]{2,1,0:T(8,128)} %mixer.1), calls=%async_computation | async-start | bytes 1048576 | tf_op jit(solution)/shard_map/all_to_all | solution.py:421
  48.6 8.0 %copy-start.7 = (s32[1,8]{1,0:T(1,128)S(1)}, s32[1,8]{1,0:T(1,128)}, u32[]{:S(2)}) copy-start(s32[1,8]{1,0:T(1,128)} %param.17) | copy-start | bytes 100
  64.1 24.4 %all-to-all-start.1 = ((f32[16,32,128]{2,1,0:T(8,128)}), f32[16,32,128]{2,1,0:T(8,128)S(1)}, u32[]{:S(2)}, u32[]{:S(2)}) async-start(f32[16,32,128]{2,1,0:T(8,128)} %broadcast_in_dim.4), calls=%async_computation.1 | async-start | bytes 524288 | tf_op jit(solution)/shard_map/all_to_all | solution.py:421
  71.4 7.1 %collective-permute-start = (bf16[16,2048]{1,0:T(8,128)(2,1)S(1)}, bf16[16,2048]{1,0:T(8,128)(2,1)S(1)}, u32[]{:S(2)}, u32[]{:S(2)}) collective-permute-start(bf16[16,2048]{1,0:T(8,128)(2,1)S(1)} %get-tuple-element.37.mine_ref), channel_id=1, source_target_pairs={{0,1},{1,2},{2,3},{3,4},{4,5},{5,6},{6,7},{7,8},{8,9},{9,10},{10,1... | collective-permute-start | bytes 196616 | tf_op jit(solution)/shard_map/ppermute | solution.py:499
  74.9 5.3 %collective-permute-start.1 = (bf16[16,2048]{1,0:T(8,128)(2,1)S(1)}, bf16[16,2048]{1,0:T(8,128)(2,1)S(1)}, u32[]{:S(2)}, u32[]{:S(2)}) collective-permute-start(bf16[16,2048]{1,0:T(8,128)(2,1)S(1)} %get-tuple-element.37.mine_ref), channel_id=1, source_target_pairs={{1,0},{2,1},{3,2},{4,3},{5,4},{6,5},{7,6},{8,7},{9,8},{10,9},{11,1... | collective-permute-start | bytes 196616 | tf_op jit(solution)/shard_map/ppermute | solution.py:501
  90.1 21.4 %all-to-all-start.2 = ((bf16[16,48,256]{2,1,0:T(8,128)(2,1)}), bf16[16,48,256]{2,1,0:T(8,128)(2,1)S(1)}, u32[]{:S(2)}, u32[]{:S(2)}) async-start(bf16[16,48,256]{2,1,0:T(8,128)(2,1)} %operator.1), calls=%async_computation.2 | async-start | bytes 786432 | tf_op jit(solution)/shard_map/all_to_all | solution.py:421
  99.0 12.5 %copy-start.4 = (f32[64,256]{1,0:T(8,128)S(1)}, f32[64,256]{1,0:T(8,128)}, u32[]{:S(2)}) copy-start(f32[64,256]{1,0:T(8,128)} %get-tuple-element.33.refs_0_) | copy-start | bytes 196612
  99.0 64.5 %copy-start.1 = (f32[1,10,32,64]{3,2,1,0:T(8,128)S(1)}, f32[1,10,32,64]{3,2,1,0:T(8,128)}, u32[]{:S(2)}) copy-start(f32[1,10,32,64]{3,2,1,0:T(8,128)} %param.13) | copy-start | bytes 245764
  105.7 57.8 %copy-start = (bf16[10,32,2048]{2,1,0:T(8,128)(2,1)S(1)}, bf16[10,32,2048]{2,1,0:T(8,128)(2,1)}, u32[]{:S(2)}) copy-start(bf16[10,32,2048]{2,1,0:T(8,128)(2,1)} %param.12) | copy-start | bytes 3932164
  105.7 66.6 %copy-start.2 = (bf16[8,32,2048]{2,1,0:T(8,128)(2,1)S(1)}, bf16[8,32,2048]{2,1,0:T(8,128)(2,1)}, u32[]{:S(2)}) copy-start(bf16[8,32,2048]{2,1,0:T(8,128)(2,1)} %param.16) | copy-start | bytes 3145732
  150.6 13.0 %all-to-all-start.5 = ((f32[16,8,256]{2,1,0:T(8,128)}), f32[16,8,256]{2,1,0:T(8,128)S(1)}, u32[]{:S(2)}, u32[]{:S(2)}) async-start(f32[16,8,256]{2,1,0:T(8,128)} %subtree.1), calls=%async_computation.5 | async-start | bytes 262144 | tf_op jit(solution)/shard_map/all_to_all | solution.py:421
  163.6 1.0 copy-start.3
  165.4 9.9 %collective-permute-start.2 = (bf16[64,2048]{1,0:T(8,128)(2,1)S(1)}, bf16[64,2048]{1,0:T(8,128)(2,1)S(1)}, u32[]{:S(2)}, u32[]{:S(2)}) collective-permute-start(bf16[64,2048]{1,0:T(8,128)(2,1)S(1)} %get-tuple-element.46.refs_2_), channel_id=1, source_target_pairs={{0,1},{1,2},{2,3},{3,4},{4,5},{5,6},{6,7},{7,8},{8,9},{9,10},{10,1... | collective-permute-start | bytes 786440 | tf_op jit(solution)/shard_map/ppermute | solution.py:550
  169.1 9.3 %collective-permute-start.3 = (bf16[64,2048]{1,0:T(8,128)(2,1)S(1)}, bf16[64,2048]{1,0:T(8,128)(2,1)S(1)}, u32[]{:S(2)}, u32[]{:S(2)}) collective-permute-start(bf16[64,2048]{1,0:T(8,128)(2,1)S(1)} %get-tuple-element.46.refs_2_), channel_id=1, source_target_pairs={{1,0},{2,1},{3,2},{4,3},{5,4},{6,5},{7,6},{8,7},{9,8},{10,9},{11,1... | collective-permute-start | bytes 786440 | tf_op jit(solution)/shard_map/ppermute | solution.py:551

commit v3 on v2

--- a/solution.py
+++ b/solution.py
@@ -159,22 +159,31 @@
         out_ref[0, :, start : start + step] = ((1.0 + scaled) * jnp.exp(-scaled)).astype(bf16)
 
 
-def distance_kernel(slots, sides, test_features, leaf_size, name, store=pltpu.HBM):
+def distance_kernel(
+    slots, sides, test_features, leaf_size, name, total, first=0, buffer=None, store=pltpu.HBM
+):
     tests = test_features.shape[1]
     operands = (*sides, test_features)
+    held = () if buffer is None else (buffer,)
+
+    def body(slots_ref, *refs):
+        distance_body(slots_ref, *refs[len(held) :])
+
     return pl.pallas_call(
-        distance_body,
-        out_shape=store((slots.shape[0], leaf_size, tests), bf16),
+        body,
+        out_shape=store((total, leaf_size, tests), bf16),
         grid_spec=pltpu.PrefetchScalarGridSpec(
             num_scalar_prefetch=1,
             grid=(slots.shape[0],),
-            in_specs=[pl.BlockSpec(a.shape, lambda i, s: (0, 0)) for a in operands],
-            out_specs=pl.BlockSpec((1, leaf_size, tests), lambda i, s: (i, 0, 0)),
+            in_specs=[pl.BlockSpec(memory_space=pl.ANY) for _ in held]
+            + [pl.BlockSpec(a.shape, lambda i, s: (0, 0)) for a in operands],
+            out_specs=pl.BlockSpec((1, leaf_size, tests), lambda i, s: (first + i, 0, 0)),
             scratch_shapes=[pltpu.VMEM((sides[0].shape[0], leaf_size), bf16)],
         ),
         compiler_params=pltpu.CompilerParams(vmem_limit_bytes=24 << 20),
+        input_output_aliases={1: 0} if held else {},
         name=name,
-    )(slots, *operands)
+    )(slots, *held, *operands)
 
 
 def node_sums(members, levels):
@@ -344,13 +353,15 @@
 
 
 def mean_body(
-    slots_ref, before_ref, mine_ref, after_ref, early_ref, late_ref, last_ref, far_ref,
+    slots_ref, before_ref, mine_ref, after_ref, values_ref, last_ref, far_ref,
     out_ref, window_ref, near_ref, *, leaf_size, factor,
 ):
     step = pl.program_id(0)
     steps = pl.num_programs(0)
-    columns = mine_ref.shape[0]
     leaf_count = mine_ref.shape[1] // leaf_size
+
+    def part_of(slot, values):
+        return jnp.dot(window_ref[slots_ref[slot]], values, preferred_element_type=f32)
 
     @pl.when(step == 0)
     def _():
@@ -360,39 +371,23 @@
                     :, leaf * leaf_size : (leaf + 1) * leaf_size
                 ]
         near_ref[...] = far_ref[...]
-
-    def part_of(slot, ref):
-        return jnp.dot(window_ref[slots_ref[slot]], ref[0], preferred_element_type=f32)
-
-    @pl.when(step < steps - 1)
-    def _():
-        near_ref[...] += part_of(step, early_ref) + part_of(steps + step, late_ref)
+        for place in range(last_ref.shape[0]):
+            near_ref[...] += part_of(steps + place, last_ref[place])
+
+    near_ref[...] += part_of(step, values_ref[0])
 
     @pl.when(step == steps - 1)
     def _():
-        near = near_ref[...] + part_of(step, early_ref) + part_of(steps + step, last_ref)
-        out_ref[...] = (near * factor).astype(bf16)
-
-
-def in_hbm(value):
-    return pltpu.with_memory_space_constraint(value, pltpu.HBM)
-
-
-def mean_kernel(slots, before, mine, after, early, late, last, far, factor):
-    steps, leaf_size, tests = early.shape
+        out_ref[...] = (near_ref[...] * factor).astype(bf16)
+
+
+def mean_kernel(slots, before, mine, after, values, last, far, factor):
+    stored, leaf_size, tests = values.shape
     columns, points = mine.shape
     whole = [before, mine, after]
 
     def fixed(array):
         return pl.BlockSpec(array.shape, lambda i, s: (0,) * array.ndim)
-
-    block = (1, leaf_size, tests)
-    final = late.shape[0] - 1
-    moving = [
-        pl.BlockSpec(block, lambda i, s: (i, 0, 0)),
-        pl.BlockSpec(block, lambda i, s: (jnp.minimum(i, final), 0, 0)),
-        pl.BlockSpec(memory_space=pltpu.VMEM),
-    ]
 
     def body(*refs):
         mean_body(*refs, leaf_size=leaf_size, factor=factor)
@@ -402,10 +397,13 @@
         out_shape=jax.ShapeDtypeStruct((columns, tests), bf16),
         grid_spec=pltpu.PrefetchScalarGridSpec(
             num_scalar_prefetch=1,
-            grid=(steps,),
+            grid=(stored,),
             in_specs=[fixed(a) for a in whole]
-            + moving
-            + [fixed(far)],
+            + [
+                pl.BlockSpec((1, leaf_size, tests), lambda i, s: (i, 0, 0)),
+                pl.BlockSpec(memory_space=pltpu.VMEM),
+                fixed(far),
+            ],
             out_specs=pl.BlockSpec((columns, tests), lambda i, s: (0, 0)),
             scratch_shapes=[
                 pltpu.VMEM((3 * points // leaf_size, columns, leaf_size), bf16),
@@ -414,7 +412,7 @@
         ),
         compiler_params=pltpu.CompilerParams(vmem_limit_bytes=24 << 20),
         name="posterior_mean",
-    )(slots, *whole, in_hbm(early), in_hbm(late), last, far)
+    )(slots, *whole, pltpu.with_memory_space_constraint(values, pltpu.HBM), last, far)
 
 
 def exchange(value, axes):
@@ -459,7 +457,9 @@
     position = high * low_count + low
     basis = cluster_basis.reshape(all_levels * rank, points)
     mixers = coupling[0]
-    half_slots = near_leaves.shape[1] // 2
+    slot_count = near_leaves.shape[1]
+    early_count, last_count = slot_count // 4, slot_count // 4
+    stored = slot_count - last_count
 
     def mixer(*refs):
         mixer_body(*refs, local_levels=local_levels, part=part)
@@ -494,14 +494,14 @@
 
     slots = near_leaves[0] - (position - 1) * leaf_count
     total = jnp.sum(spread, axis=0)[:, low_width:]
-    early_slots, train_rows, total = tie(slots[:half_slots], train_rows, total)
+    early_slots, train_rows, total = tie(slots[:early_count], train_rows, total)
     sides = (
         lax.ppermute(train_rows, panel_axes, forward),
         train_rows,
         lax.ppermute(train_rows, panel_axes, backward),
     )
     high_spread = gathered(total, "z")
-    early = distance_kernel(early_slots, sides, test_rows, leaf_size, "near_early")
+    early = distance_kernel(early_slots, sides, test_rows, leaf_size, "near_early", stored)
     early, high_spread = tie(early, high_spread)
 
     def operator(*refs):
@@ -510,9 +510,11 @@
     operators = whole_call(
         operator, jax.ShapeDtypeStruct((low_count, 3 * part, width), bf16), "operator", 1
     )(place, spread, high_spread)
-    late_slots, operators = tie(slots[half_slots:-1], operators)
+    late_slots, operators = tie(slots[early_count:stored], operators)
     operators = exchange(operators, low_axes)
-    late = distance_kernel(late_slots, sides, test_rows, leaf_size, "near_late")
+    late = distance_kernel(
+        late_slots, sides, test_rows, leaf_size, "near_late", stored, early_count, early
+    )
     late, operators = tie(late, operators)
 
     def eliminate(*refs):
@@ -543,9 +545,10 @@
         ],
         "weights",
     )(sums, state, basis, mixers)
-    last_slot, weights = tie(slots[-1:], weights)
+    last_slots, weights = tie(slots[stored:], weights)
     last = distance_kernel(
-        last_slot, sides, test_rows, leaf_size, "near_last", jax.ShapeDtypeStruct
+        last_slots, sides, test_rows, leaf_size, "near_last", last_count,
+        store=jax.ShapeDtypeStruct,
     )
     before = lax.ppermute(weights, panel_axes, forward)
     after = lax.ppermute(weights, panel_axes, backward)
@@ -557,7 +560,7 @@
     far = whole_call(distant, jax.ShapeDtypeStruct((columns, points), f32), "far")(
         joined, operators, test_basis.reshape(width, -1)
     )
-    return mean_kernel(slots, before, weights, after, early, late, last, far, factor)
+    return mean_kernel(slots, before, weights, after, late, last, far, factor)
 
 
 def solution(mesh):

time: 188 us -> 184 us (0.979)
  blocking collectives: 36.8 us -> 47.8 us
  starting transfers between devices: 80.5 us -> 71.7 us
  waiting for transfers between devices: 24 us -> 16.9 us
    all_to_all x2 -> x3, blocking collectives: 36.8 us -> 47.8 us  [exchange(): return lax.all_to_all(value, axes, 0, 0)]
    all_to_all x4 -> x3, waiting for transfers between devices: 19.1 us -> 9.44 us  [exchange(): return lax.all_to_all(value, axes, 0, 0)]
    all_to_all x4 -> x3, starting transfers between devices: 66.8 us -> 59.6 us  [exchange(): return lax.all_to_all(value, axes, 0, 0)]
    ppermute x1, waiting for transfers between devices: 0.19 us -> 5.08 us  [shards(): lax.ppermute(train_rows, panel_axes, forward)]
    ppermute x1, waiting for transfers between devices: 3.02 us -> 0.01 us  [shards(): after = lax.ppermute(weights, panel_axes, backward)]
    ppermute x1, waiting for transfers between devices: 0.01 us -> 2.38 us  [shards(): before = lax.ppermute(weights, panel_axes, forward)]
  transfers between devices with their start and end apart: 8 -> 7, of which waited for: 6 -> 4; matrix products, arithmetic and copies ran while one was open for 0% -> 0% of each run, Pallas kernels for 14% -> 14%
where the time goes in v3:
time: 184 us; the launch traced here: 183 us
  starting transfers between devices  71.7 us (39%)
  blocking collectives  47.8 us (26%)
  Pallas kernels  42.9 us (23%)
  waiting for transfers between devices  16.9 us (9%)
  local copies, waits for them, and re-layouts  3.39 us (2%)
    all_to_all x3, starting transfers between devices, exchange(): return lax.all_to_all(value, axes, 0, 0)  59.6 us
    all_to_all x3, blocking collectives, exchange(): return lax.all_to_all(value, axes, 0, 0)  47.8 us
    pallas_call x3, Pallas kernels, distance_kernel(): pl.pallas_call(body, out_shape=store((total, leaf_size, tests), bf16), gr...  17.1 us
    pallas_call x8, Pallas kernels, call(): pl.pallas_call(body, out_shape=out_shape, in_specs=specs, out_specs=out_s...  16.5 us
    all_to_all x3, waiting for transfers between devices, exchange(): return lax.all_to_all(value, axes, 0, 0)  9.44 us
    pallas_call x1, Pallas kernels, mean_kernel(): pl.pallas_call(body, out_shape=jax.ShapeDtypeStruct((columns, tests), bf1...  9.31 us
    ppermute x1, waiting for transfers between devices, shards(): lax.ppermute(train_rows, panel_axes, forward)  5.08 us
    ppermute x1, starting transfers between devices, shards(): lax.ppermute(train_rows, panel_axes, backward)  4.11 us
  transfers between devices with their start and end apart: 7, of which 4 were waited for; matrix products, arithmetic and copies ran while one was open for 0% of the time, Pallas kernels for 14%

profile of v3, /device:TPU:65, one launch (start us, length us, event | category | flops | bytes accessed | tf_op | source)
XLA Modules:
  0.0 183.0 jit_solution(10353616305141666469)
XLA Ops:
  0.0 0.0 copy-start.7
  0.0 3.6 %mixer.1 = f32[16,32,256]{2,1,0:T(8,128)} custom-call(bf16[320,2048]{1,0:T(8,128)(2,1)} %bitcast.13, f32[10,32,64]{2,1,0:T(8,128)} %bitcast.16), custom_call_target="tpu_custom_call" | custom-call | tf_op jit(solution)/shard_map/mixer/pallas_call | solution.py:49
  3.6 44.9 %all-to-all-start = ((f32[16,32,256]{2,1,0:T(8,128)}), f32[16,32,256]{2,1,0:T(8,128)S(1)}, u32[]{:S(2)}, u32[]{:S(2)}) async-start(f32[16,32,256]{2,1,0:T(8,128)} %mixer.1), calls=%async_computation | async-start | bytes 1048576 | tf_op jit(solution)/shard_map/all_to_all | solution.py:419
  48.6 0.0 copy-start.5
  48.6 0.7 copy-done.5
  49.3 0.0 copy-start.6
  49.3 0.7 copy-done.6
  50.0 0.2 points.1
  50.2 7.8 %local.1 = (f32[64,2048]{1,0:T(8,128)}, f32[64,256]{1,0:T(8,128)}) custom-call(bf16[64,2048]{1,0:T(8,128)(2,1)} %targets_ref.1, s32[1,2048]{1,0:T(1,128)} %order_ref, bf16[4,512,512]{2,1,0:T(8,128)(2,1)} %inverse_ref.1, bf16[320,2048]{1,0:T(8,128)(2,1)} %bitcast.14, f32[10,32,64]{2,1,0:T(8,128)} %bitcast.17), custom_call_target="tpu_custom_call" | custom-call | tf_op jit(solution)/shard_map/local/pallas_call | solution.py:49
  58.0 0.0 copy-done.7
  58.0 0.1 slice_bitcast_fusion
  58.1 5.3 %all-to-all-done.refs_1_ = f32[16,32,256]{2,1,0:T(8,128)S(1)} async-done(((f32[16,32,256]{2,1,0:T(8,128)}), f32[16,32,256]{2,1,0:T(8,128)S(1)}, u32[]{:S(2)}, u32[]{:S(2)}) %all-to-all-start) | async-done | bytes 524320 | tf_op jit(solution)/shard_map/all_to_all | solution.py:419
  63.4 0.7 broadcast_in_dim.4
  64.1 7.2 %all-to-all-start.1 = ((f32[16,32,128]{2,1,0:T(8,128)}), f32[16,32,128]{2,1,0:T(8,128)S(1)}, u32[]{:S(2)}, u32[]{:S(2)}) async-start(f32[16,32,128]{2,1,0:T(8,128)} %broadcast_in_dim.4), calls=%async_computation.1 | async-start | bytes 524288 | tf_op jit(solution)/shard_map/all_to_all | solution.py:419
  71.3 0.1 slice_bitcast_fusion.1.slots_ref
  71.4 4.1 %collective-permute-start.1 = (bf16[16,2048]{1,0:T(8,128)(2,1)S(1)}, bf16[16,2048]{1,0:T(8,128)(2,1)S(1)}, u32[]{:S(2)}, u32[]{:S(2)}) collective-permute-start(bf16[16,2048]{1,0:T(8,128)(2,1)S(1)} %get-tuple-element.37.refs_1_.refs_2_), channel_id=1, source_target_pairs={{1,0},{2,1},{3,2},{4,3},{5,4},{6,5},{7,6},{8,7},{9,8},{10,9},{11,1... | collective-permute-start | bytes 196616 | tf_op jit(solution)/shard_map/ppermute | solution.py:501
  75.5 2.0 %collective-permute-start = (bf16[16,2048]{1,0:T(8,128)(2,1)S(1)}, bf16[16,2048]{1,0:T(8,128)(2,1)S(1)}, u32[]{:S(2)}, u32[]{:S(2)}) collective-permute-start(bf16[16,2048]{1,0:T(8,128)(2,1)S(1)} %get-tuple-element.37.refs_1_.refs_2_), channel_id=1, source_target_pairs={{0,1},{1,2},{2,3},{3,4},{4,5},{5,6},{6,7},{7,8},{8,9},{9,10},{10,1... | collective-permute-start | bytes 196616 | tf_op jit(solution)/shard_map/ppermute | solution.py:499
  77.5 0.1 pad_add_fusion.refs_0_
  77.6 0.0 collective-permute-done.1.refs_2_.refs_3_
  77.6 5.1 %collective-permute-done.refs_0_.refs_1_ = bf16[16,2048]{1,0:T(8,128)(2,1)S(1)} collective-permute-done((bf16[16,2048]{1,0:T(8,128)(2,1)S(1)}, bf16[16,2048]{1,0:T(8,128)(2,1)S(1)}, u32[]{:S(2)}, u32[]{:S(2)}) %collective-permute-start) | collective-permute-done | bytes 65568 | tf_op jit(solution)/shard_map/ppermute | solution.py:499
  82.7 5.1 %near_early.1.refs_0_ = bf16[6,512,2048]{2,1,0:T(8,128)(2,1)} custom-call(s32[2]{0:T(128)S(1)} %get-tuple-element.36.slots_ref, bf16[16,2048]{1,0:T(8,128)(2,1)S(1)} %collective-permute-done.refs_0_.refs_1_, bf16[16,2048]{1,0:T(8,128)(2,1)S(1)} %get-tuple-element.37.refs_1_.refs_2_, bf16[16,2048]{1,0:T(8,128)(2,1)S(1)} %collective-permute-done.1.refs_2_.refs_3_, ...), custom_call_target="tpu_custom_call" | custom-call | tf_op jit(solution)/shard_map/near_early/pallas_call | solution.py:172
  87.7 0.0 all-to-all-done.1.refs_2_
  87.7 1.6 operator.1
  89.4 7.5 %all-to-all-start.2 = ((bf16[16,48,256]{2,1,0:T(8,128)(2,1)}), bf16[16,48,256]{2,1,0:T(8,128)(2,1)S(1)}, u32[]{:S(2)}, u32[]{:S(2)}) async-start(bf16[16,48,256]{2,1,0:T(8,128)(2,1)} %operator.1), calls=%async_computation.2 | async-start | bytes 786432 | tf_op jit(solution)/shard_map/all_to_all | solution.py:419
  96.9 0.0 copy-start.4
  96.9 0.0 copy-start
  96.9 0.0 copy-start.1
  96.9 0.0 copy-start.2
  96.9 8.3 %near_late.1.refs_4_ = bf16[6,512,2048]{2,1,0:T(8,128)(2,1)} custom-call(s32[4]{0:T(128)S(1)} %slice_bitcast_fusion.1.slots_ref, bf16[6,512,2048]{2,1,0:T(8,128)(2,1)} %near_early.1.refs_0_, bf16[16,2048]{1,0:T(8,128)(2,1)S(1)} %collective-permute-done.refs_0_.refs_1_, ...), custom_call_target="tpu_custom_call", output_to_operand_aliasing={{}: (1, {})} | custom-call | tf_op jit(solution)/shard_map/near_late/pallas_call | solution.py:172
  105.2 4.1 %all-to-all-done.2.refs_1_ = bf16[16,48,256]{2,1,0:T(8,128)(2,1)S(1)} async-done(((bf16[16,48,256]{2,1,0:T(8,128)(2,1)}), bf16[16,48,256]{2,1,0:T(8,128)(2,1)S(1)}, u32[]{:S(2)}, u32[]{:S(2)}) %all-to-all-start.2) | async-done | bytes 393248 | tf_op jit(solution)/shard_map/all_to_all | solution.py:419
  109.3 0.0 copy-done.4
  109.3 1.1 eliminate.1
  110.4 11.9 %all_to_all.30.refs_1_ = f32[16,4,256]{2,1,0:T(4,128)S(1)} all-to-all(f32[16,4,256]{2,1,0:T(4,128)S(1)} %eliminate.1), channel_id=1, replica_groups=mesh['grp'=2,'z'=16,'core'=2,'sub'=8] {'core','sub'}, dimensions={0} | all-to-all | bytes 131072 | tf_op jit(solution)/shard_map/all_to_all | solution.py:419
  122.3 23.9 %all_to_all.31.refs_2_ = f32[16,4,128]{2,1,0:T(4,128)S(1)} all-to-all(f32[16,4,128]{2,1,0:T(4,128)S(1)} %broadcast_in_dim.5), channel_id=1, replica_groups=mesh['grp'=2,'z'=16,'core'=2,'sub'=8] {'z'}, dimensions={0} | all-to-all | bytes 65536 | tf_op jit(solution)/shard_map/all_to_all | solution.py:419
  146.2 0.6 subtree.1
  146.7 12.1 %all_to_all.32.refs_0_ = f32[16,8,256]{2,1,0:T(8,128)S(1)} all-to-all(f32[16,8,256]{2,1,0:T(8,128)S(1)} %subtree.1), channel_id=1, replica_groups=mesh['grp'=2,'z'=16,'core'=2,'sub'=8] {'core','sub'}, dimensions={0} | all-to-all | bytes 262144 | tf_op jit(solution)/shard_map/all_to_all | solution.py:419
  158.8 0.0 copy-done
  158.8 0.0 copy-done.1
  158.8 1.0 copy-done.3
  159.9 0.8 weights.1
  160.7 4.1 %collective-permute-start.3 = (bf16[64,2048]{1,0:T(8,128)(2,1)S(1)}, bf16[64,2048]{1,0:T(8,128)(2,1)S(1)}, u32[]{:S(2)}, u32[]{:S(2)}) collective-permute-start(bf16[64,2048]{1,0:T(8,128)(2,1)S(1)} %get-tuple-element.47.refs_2_), channel_id=1, source_target_pairs={{1,0},{2,1},{3,2},{4,3},{5,4},{6,5},{7,6},{8,7},{9,8},{10,9},{11,1... | collective-permute-start | bytes 786440 | tf_op jit(solution)/shard_map/ppermute | solution.py:554
  164.8 2.0 %collective-permute-start.2 = (bf16[64,2048]{1,0:T(8,128)(2,1)S(1)}, bf16[64,2048]{1,0:T(8,128)(2,1)S(1)}, u32[]{:S(2)}, u32[]{:S(2)}) collective-permute-start(bf16[64,2048]{1,0:T(8,128)(2,1)S(1)} %get-tuple-element.47.refs_2_), channel_id=1, source_target_pairs={{0,1},{1,2},{2,3},{3,4},{4,5},{5,6},{6,7},{7,8},{8,9},{9,10},{10,1... | collective-permute-start | bytes 786440 | tf_op jit(solution)/shard_map/ppermute | solution.py:553
  166.8 0.0 copy-done.2
  166.8 0.8 far.1.refs_6_
  167.6 3.7 %near_last.1.refs_5_ = bf16[2,512,2048]{2,1,0:T(8,128)(2,1)S(1)} custom-call(s32[2]{0:T(128)S(1)} %get-tuple-element.49.slots_ref, bf16[16,2048]{1,0:T(8,128)(2,1)S(1)} %collective-permute-done.refs_0_.refs_1_, bf16[16,2048]{1,0:T(8,128)(2,1)S(1)} %get-tuple-element.37.refs_1_.refs_2_, bf16[16,2048]{1,0:T(8,128)(2,1)S(1)} %collective-permute-done.1.refs_2_.refs_3_, ...), custom_call_target="tpu_custom_call" | custom-call | tf_op jit(solution)/shard_map/near_last/pallas_call | solution.py:172
  171.3 0.0 collective-permute-done.3.refs_3_
  171.3 2.4 %collective-permute-done.2.refs_1_ = bf16[64,2048]{1,0:T(8,128)(2,1)S(1)} collective-permute-done((bf16[64,2048]{1,0:T(8,128)(2,1)S(1)}, bf16[64,2048]{1,0:T(8,128)(2,1)S(1)}, u32[]{:S(2)}, u32[]{:S(2)}) %collective-permute-start.2) | collective-permute-done | bytes 262176 | tf_op jit(solution)/shard_map/ppermute | solution.py:553
  173.7 9.3 %posterior_mean.1 = bf16[64,2048]{1,0:T(8,128)(2,1)} custom-call(s32[8]{0:T(128)S(1)} %fusion.refs_0_, bf16[64,2048]{1,0:T(8,128)(2,1)S(1)} %collective-permute-done.2.refs_1_, bf16[64,2048]{1,0:T(8,128)(2,1)S(1)} %get-tuple-element.47.refs_2_, bf16[64,2048]{1,0:T(8,128)(2,1)S(1)} %collective-permute-done.3.refs_3_, bf16[6,512,2048]{2,1,0:T(8,128)(2,1)} %near_late.1.refs_4_, ...), custom_call_target="tpu_custom_call" | custom-call | tf_op jit(solution)/shard_map/posterior_mean/pallas_call | solution.py:395
  (8 shorter events, 0.1 us)
Async XLA Ops:
  0.0 58.0 %copy-start.7 = (s32[1,8]{1,0:T(1,128)S(1)}, s32[1,8]{1,0:T(1,128)}, u32[]{:S(2)}) copy-start(s32[1,8]{1,0:T(1,128)} %param.17) | copy-start | bytes 100
  3.6 59.7 %all-to-all-start = ((f32[16,32,256]{2,1,0:T(8,128)}), f32[16,32,256]{2,1,0:T(8,128)S(1)}, u32[]{:S(2)}, u32[]{:S(2)}) async-start(f32[16,32,256]{2,1,0:T(8,128)} %mixer.1), calls=%async_computation | async-start | bytes 1048576 | tf_op jit(solution)/shard_map/all_to_all | solution.py:419
  48.6 0.7 copy-start.5
  49.3 0.7 copy-start.6
  64.1 23.6 %all-to-all-start.1 = ((f32[16,32,128]{2,1,0:T(8,128)}), f32[16,32,128]{2,1,0:T(8,128)S(1)}, u32[]{:S(2)}, u32[]{:S(2)}) async-start(f32[16,32,128]{2,1,0:T(8,128)} %broadcast_in_dim.4), calls=%async_computation.1 | async-start | bytes 524288 | tf_op jit(solution)/shard_map/all_to_all | solution.py:419
  71.4 6.2 %collective-permute-start.1 = (bf16[16,2048]{1,0:T(8,128)(2,1)S(1)}, bf16[16,2048]{1,0:T(8,128)(2,1)S(1)}, u32[]{:S(2)}, u32[]{:S(2)}) collective-permute-start(bf16[16,2048]{1,0:T(8,128)(2,1)S(1)} %get-tuple-element.37.refs_1_.refs_2_), channel_id=1, source_target_pairs={{1,0},{2,1},{3,2},{4,3},{5,4},{6,5},{7,6},{8,7},{9,8},{10,9},{11,1... | collective-permute-start | bytes 196616 | tf_op jit(solution)/shard_map/ppermute | solution.py:501
  75.5 7.1 %collective-permute-start = (bf16[16,2048]{1,0:T(8,128)(2,1)S(1)}, bf16[16,2048]{1,0:T(8,128)(2,1)S(1)}, u32[]{:S(2)}, u32[]{:S(2)}) collective-permute-start(bf16[16,2048]{1,0:T(8,128)(2,1)S(1)} %get-tuple-element.37.refs_1_.refs_2_), channel_id=1, source_target_pairs={{0,1},{1,2},{2,3},{3,4},{4,5},{5,6},{6,7},{7,8},{8,9},{9,10},{10,1... | collective-permute-start | bytes 196616 | tf_op jit(solution)/shard_map/ppermute | solution.py:499
  89.4 20.0 %all-to-all-start.2 = ((bf16[16,48,256]{2,1,0:T(8,128)(2,1)}), bf16[16,48,256]{2,1,0:T(8,128)(2,1)S(1)}, u32[]{:S(2)}, u32[]{:S(2)}) async-start(bf16[16,48,256]{2,1,0:T(8,128)(2,1)} %operator.1), calls=%async_computation.2 | async-start | bytes 786432 | tf_op jit(solution)/shard_map/all_to_all | solution.py:419
  96.9 12.5 %copy-start.4 = (f32[64,256]{1,0:T(8,128)S(1)}, f32[64,256]{1,0:T(8,128)}, u32[]{:S(2)}) copy-start(f32[64,256]{1,0:T(8,128)} %get-tuple-element.33.refs_0_) | copy-start | bytes 196612
  96.9 61.9 %copy-start = (bf16[10,32,2048]{2,1,0:T(8,128)(2,1)S(1)}, bf16[10,32,2048]{2,1,0:T(8,128)(2,1)}, u32[]{:S(2)}) copy-start(bf16[10,32,2048]{2,1,0:T(8,128)(2,1)} %param.12) | copy-start | bytes 3932164
  96.9 61.9 %copy-start.1 = (f32[1,10,32,64]{3,2,1,0:T(8,128)S(1)}, f32[1,10,32,64]{3,2,1,0:T(8,128)}, u32[]{:S(2)}) copy-start(f32[1,10,32,64]{3,2,1,0:T(8,128)} %param.13) | copy-start | bytes 245764
  96.9 69.9 %copy-start.2 = (bf16[8,32,2048]{2,1,0:T(8,128)(2,1)S(1)}, bf16[8,32,2048]{2,1,0:T(8,128)(2,1)}, u32[]{:S(2)}) copy-start(bf16[8,32,2048]{2,1,0:T(8,128)(2,1)} %param.16) | copy-start | bytes 3145732
  158.8 1.0 copy-start.3
  160.7 10.6 %collective-permute-start.3 = (bf16[64,2048]{1,0:T(8,128)(2,1)S(1)}, bf16[64,2048]{1,0:T(8,128)(2,1)S(1)}, u32[]{:S(2)}, u32[]{:S(2)}) collective-permute-start(bf16[64,2048]{1,0:T(8,128)(2,1)S(1)} %get-tuple-element.47.refs_2_), channel_id=1, source_target_pairs={{1,0},{2,1},{3,2},{4,3},{5,4},{6,5},{7,6},{8,7},{9,8},{10,9},{11,1... | collective-permute-start | bytes 786440 | tf_op jit(solution)/shard_map/ppermute | solution.py:554
  164.8 8.9 %collective-permute-start.2 = (bf16[64,2048]{1,0:T(8,128)(2,1)S(1)}, bf16[64,2048]{1,0:T(8,128)(2,1)S(1)}, u32[]{:S(2)}, u32[]{:S(2)}) collective-permute-start(bf16[64,2048]{1,0:T(8,128)(2,1)S(1)} %get-tuple-element.47.refs_2_), channel_id=1, source_target_pairs={{0,1},{1,2},{2,3},{3,4},{4,5},{5,6},{6,7},{7,8},{8,9},{9,10},{10,1... | collective-permute-start | bytes 786440 | tf_op jit(solution)/shard_map/ppermute | solution.py:553

commit v4 on v3

--- a/solution.py
+++ b/solution.py
@@ -78,7 +78,7 @@
         out_ref[...] = rows_ref[...].astype(bf16)
 
 
-def mixer_body(basis_ref, coupling_ref, out_ref, *, local_levels, part):
+def mixer_body(basis_ref, coupling_ref, out_ref, *, local_levels):
     rank = coupling_ref.shape[1]
     width = basis_ref.shape[0] - local_levels * rank
     points = basis_ref.shape[1]
@@ -86,15 +86,18 @@
     gram = lax.dot_general(basis, basis, rows_by_rows, preferred_element_type=f32)
     level = lax.broadcasted_iota(jnp.int32, (1, width), 1) // rank
     gram = gram * (lax.exp2(-0.5 * level.astype(f32)) / math.sqrt(points))
+    piece = out_ref.shape[1] // 4
     for depth in range(width // rank):
-        piece = gram[depth * rank : (depth + 1) * rank, :]
-        product = full_dot(coupling_ref[local_levels + depth], piece, columns_by_columns)
+        rows = gram[depth * rank : (depth + 1) * rank, :]
+        product = full_dot(coupling_ref[local_levels + depth], rows, columns_by_columns)
+        upper, group = divmod(depth, width // rank // 2)
         for half in range(2):
-            for block in range(rank // part):
-                start = half * rank + block * part
-                out_ref[depth * (rank // part) + block, half * part : (half + 1) * part, :] = (
-                    product[start : start + part, :]
-                )
+            for block in range(rank // piece):
+                start = half * rank + block * piece
+                row = (2 * half + upper) * piece
+                out_ref[group * (rank // piece) + block, row : row + piece, :] = product[
+                    start : start + piece, :
+                ]
 
 
 def local_body(targets_ref, order_ref, inverse_ref, basis_ref, coupling_ref, state_ref, terms_ref):
@@ -159,31 +162,22 @@
         out_ref[0, :, start : start + step] = ((1.0 + scaled) * jnp.exp(-scaled)).astype(bf16)
 
 
-def distance_kernel(
-    slots, sides, test_features, leaf_size, name, total, first=0, buffer=None, store=pltpu.HBM
-):
+def distance_kernel(slots, sides, test_features, leaf_size, name, store):
     tests = test_features.shape[1]
     operands = (*sides, test_features)
-    held = () if buffer is None else (buffer,)
-
-    def body(slots_ref, *refs):
-        distance_body(slots_ref, *refs[len(held) :])
-
     return pl.pallas_call(
-        body,
-        out_shape=store((total, leaf_size, tests), bf16),
+        distance_body,
+        out_shape=store((slots.shape[0], leaf_size, tests), bf16),
         grid_spec=pltpu.PrefetchScalarGridSpec(
             num_scalar_prefetch=1,
             grid=(slots.shape[0],),
-            in_specs=[pl.BlockSpec(memory_space=pl.ANY) for _ in held]
-            + [pl.BlockSpec(a.shape, lambda i, s: (0, 0)) for a in operands],
-            out_specs=pl.BlockSpec((1, leaf_size, tests), lambda i, s: (first + i, 0, 0)),
+            in_specs=[pl.BlockSpec(a.shape, lambda i, s: (0, 0)) for a in operands],
+            out_specs=pl.BlockSpec((1, leaf_size, tests), lambda i, s: (i, 0, 0)),
             scratch_shapes=[pltpu.VMEM((sides[0].shape[0], leaf_size), bf16)],
         ),
         compiler_params=pltpu.CompilerParams(vmem_limit_bytes=24 << 20),
-        input_output_aliases={1: 0} if held else {},
         name=name,
-    )(slots, *held, *operands)
+    )(slots, *operands)
 
 
 def node_sums(members, levels):
@@ -218,29 +212,33 @@
     low_width = width - high_width
     low_levels = low_count.bit_length() - 1
     high_levels = high_count.bit_length() - 1
-    row_level = place_ref[0] * part // rank
+    piece = part // 2
+    row = lax.broadcasted_iota(jnp.int32, (part, width), 0)
+    row_level = place_ref[0] * piece // rank + low_levels * (row // piece)
     lane_level = lax.broadcasted_iota(jnp.int32, (part, width), 1) // rank
     pair_level = jnp.minimum(lane_level, row_level)
-    upper = pair_level >= low_levels
     below = lane_level < row_level
     equal = lane_level == row_level
-    blank = jnp.zeros((part, low_width), f32)
+    blank = jnp.zeros((piece, low_width), f32)
     trees = []
     highs = []
     for half in range(2):
         rows_here = slice(half * part, (half + 1) * part)
         trees.append(node_sums([spread_ref[p, rows_here, :] for p in range(low_count)], low_levels))
         own, sibling = chain_sums(
-            [high_ref[p, rows_here, :] for p in range(high_count)], place_ref[1], high_levels
+            [high_ref[p, half * piece : (half + 1) * piece, :] for p in range(high_count)],
+            place_ref[1],
+            high_levels,
         )
         picks = []
         for values in (own, sibling):
             pick = values[0]
             for level in range(1, high_levels):
                 pick = jnp.where(
-                    pair_level[:, low_width:] == low_levels + level, values[level], pick
+                    pair_level[piece:, low_width:] == low_levels + level, values[level], pick
                 )
-            picks.append(jnp.concatenate([blank, pick], axis=1))
+            pick = jnp.concatenate([blank, pick], axis=1)
+            picks.append(jnp.concatenate([jnp.zeros_like(pick), pick], axis=0))
         highs.append(picks)
     for p in range(low_count):
         own, sibling = [], []
@@ -263,10 +261,16 @@
 def operators_of(ref, rank):
     count, rows, width = ref.shape
     part = rows // 3
-    first, rest, second = (
-        ref[:, i * part : (i + 1) * part, :].reshape(count * part, width).astype(f32)
-        for i in range(3)
-    )
+
+    def natural(block):
+        value = ref[:, block * part : (block + 1) * part, :].astype(f32)
+        halves = [
+            value[:, half * part // 2 : (half + 1) * part // 2, :].reshape(-1, width)
+            for half in range(2)
+        ]
+        return jnp.concatenate(halves, axis=0)
+
+    first, rest, second = (natural(block) for block in range(3))
     first = first + rest
     row_level = lax.broadcasted_iota(jnp.int32, (width, width), 0) // rank
     lane_level = lax.broadcasted_iota(jnp.int32, (width, width), 1) // rank
@@ -354,65 +358,65 @@
 
 def mean_body(
     slots_ref, before_ref, mine_ref, after_ref, values_ref, last_ref, far_ref,
-    out_ref, window_ref, near_ref, *, leaf_size, factor,
+    out_ref, window_ref, near_ref, held_ref, arrived, *, leaf_size, factor,
 ):
-    step = pl.program_id(0)
-    steps = pl.num_programs(0)
+    stored = values_ref.shape[0]
     leaf_count = mine_ref.shape[1] // leaf_size
+    copies = [
+        pltpu.make_async_copy(values_ref.at[slot], held_ref.at[slot], arrived.at[slot])
+        for slot in range(stored)
+    ]
+    for copy in copies:
+        copy.start()
+    for side, ref in enumerate((before_ref, mine_ref, after_ref)):
+        for leaf in range(leaf_count):
+            window_ref[side * leaf_count + leaf] = ref[:, leaf * leaf_size : (leaf + 1) * leaf_size]
 
     def part_of(slot, values):
         return jnp.dot(window_ref[slots_ref[slot]], values, preferred_element_type=f32)
 
-    @pl.when(step == 0)
-    def _():
-        for side, ref in enumerate((before_ref, mine_ref, after_ref)):
-            for leaf in range(leaf_count):
-                window_ref[side * leaf_count + leaf] = ref[
-                    :, leaf * leaf_size : (leaf + 1) * leaf_size
-                ]
-        near_ref[...] = far_ref[...]
-        for place in range(last_ref.shape[0]):
-            near_ref[...] += part_of(steps + place, last_ref[place])
-
-    near_ref[...] += part_of(step, values_ref[0])
-
-    @pl.when(step == steps - 1)
-    def _():
-        out_ref[...] = (near_ref[...] * factor).astype(bf16)
+    near_ref[...] = far_ref[...]
+    for place in range(last_ref.shape[0]):
+        near_ref[...] += part_of(stored + place, last_ref[place])
+    for slot in range(stored):
+        copies[slot].wait()
+        near_ref[...] += part_of(slot, held_ref[slot])
+    out_ref[...] = (near_ref[...] * factor).astype(bf16)
 
 
 def mean_kernel(slots, before, mine, after, values, last, far, factor):
     stored, leaf_size, tests = values.shape
     columns, points = mine.shape
-    whole = [before, mine, after]
-
-    def fixed(array):
-        return pl.BlockSpec(array.shape, lambda i, s: (0,) * array.ndim)
 
     def body(*refs):
         mean_body(*refs, leaf_size=leaf_size, factor=factor)
 
+    vmem = pl.BlockSpec(memory_space=pltpu.VMEM)
     return pl.pallas_call(
         body,
         out_shape=jax.ShapeDtypeStruct((columns, tests), bf16),
-        grid_spec=pltpu.PrefetchScalarGridSpec(
-            num_scalar_prefetch=1,
-            grid=(stored,),
-            in_specs=[fixed(a) for a in whole]
-            + [
-                pl.BlockSpec((1, leaf_size, tests), lambda i, s: (i, 0, 0)),
-                pl.BlockSpec(memory_space=pltpu.VMEM),
-                fixed(far),
-            ],
-            out_specs=pl.BlockSpec((columns, tests), lambda i, s: (0, 0)),
-            scratch_shapes=[
-                pltpu.VMEM((3 * points // leaf_size, columns, leaf_size), bf16),
-                pltpu.VMEM((columns, tests), f32),
-            ],
-        ),
+        in_specs=[
+            pl.BlockSpec(memory_space=pltpu.SMEM),
+            vmem,
+            vmem,
+            vmem,
+            pl.BlockSpec(memory_space=pl.ANY),
+            vmem,
+            vmem,
+        ],
+        out_specs=vmem,
+        scratch_shapes=[
+            pltpu.VMEM((3 * points // leaf_size, columns, leaf_size), bf16),
+            pltpu.VMEM((columns, tests), f32),
+            pltpu.VMEM(values.shape, bf16),
+            pltpu.SemaphoreType.DMA((stored,)),
+        ],
         compiler_params=pltpu.CompilerParams(vmem_limit_bytes=24 << 20),
         name="posterior_mean",
-    )(slots, *whole, pltpu.with_memory_space_constraint(values, pltpu.HBM), last, far)
+    )(
+        slots, before, mine, after,
+        pltpu.with_memory_space_constraint(values, pltpu.HBM), last, far,
+    )
 
 
 def exchange(value, axes):
@@ -458,11 +462,11 @@
     basis = cluster_basis.reshape(all_levels * rank, points)
     mixers = coupling[0]
     slot_count = near_leaves.shape[1]
-    early_count, last_count = slot_count // 4, slot_count // 4
+    last_count = slot_count // 4
     stored = slot_count - last_count
 
     def mixer(*refs):
-        mixer_body(*refs, local_levels=local_levels, part=part)
+        mixer_body(*refs, local_levels=local_levels)
 
     effect = whole_call(
         mixer, jax.ShapeDtypeStruct((low_count, 2 * part, width), f32), "mixer", limit=None
@@ -493,16 +497,16 @@
     terms, spread = tie(terms, spread)
 
     slots = near_leaves[0] - (position - 1) * leaf_count
-    total = jnp.sum(spread, axis=0)[:, low_width:]
-    early_slots, train_rows, total = tie(slots[:early_count], train_rows, total)
+    total = jnp.sum(spread, axis=0).reshape(2, part, width)[:, part // 2 :, low_width:]
+    total = total.reshape(part, width - low_width)
+    train_rows, total = tie(train_rows, total)
     sides = (
         lax.ppermute(train_rows, panel_axes, forward),
         train_rows,
         lax.ppermute(train_rows, panel_axes, backward),
     )
     high_spread = gathered(total, "z")
-    early = distance_kernel(early_slots, sides, test_rows, leaf_size, "near_early", stored)
-    early, high_spread = tie(early, high_spread)
+    *sides, high_spread = tie(*sides, high_spread)
 
     def operator(*refs):
         operator_body(*refs, rank=rank)
@@ -510,11 +514,9 @@
     operators = whole_call(
         operator, jax.ShapeDtypeStruct((low_count, 3 * part, width), bf16), "operator", 1
     )(place, spread, high_spread)
-    late_slots, operators = tie(slots[early_count:stored], operators)
+    late_slots, operators = tie(slots[:stored], operators)
     operators = exchange(operators, low_axes)
-    late = distance_kernel(
-        late_slots, sides, test_rows, leaf_size, "near_late", stored, early_count, early
-    )
+    late = distance_kernel(late_slots, sides, test_rows, leaf_size, "near_late", pltpu.HBM)
     late, operators = tie(late, operators)
 
     def eliminate(*refs):
@@ -547,8 +549,7 @@
     )(sums, state, basis, mixers)
     last_slots, weights = tie(slots[stored:], weights)
     last = distance_kernel(
-        last_slots, sides, test_rows, leaf_size, "near_last", last_count,
-        store=jax.ShapeDtypeStruct,
+        last_slots, sides, test_rows, leaf_size, "near_last", jax.ShapeDtypeStruct
     )
     before = lax.ppermute(weights, panel_axes, forward)
     after = lax.ppermute(weights, panel_axes, backward)

time: 184 us -> 176 us (0.957)
  blocking collectives: 47.8 us -> 32.4 us
  starting transfers between devices: 71.7 us -> 80.1 us
  Pallas kernels: 42.9 us -> 38.8 us
  waiting for transfers between devices: 16.9 us -> 19.7 us
    all_to_all x3 -> x2, blocking collectives: 47.8 us -> 32.4 us  [exchange(): return lax.all_to_all(value, axes, 0, 0)]
    all_to_all x3 -> x4, waiting for transfers between devices: 9.44 us -> 16.5 us  [exchange(): return lax.all_to_all(value, axes, 0, 0)]
    all_to_all x3 -> x4, starting transfers between devices: 59.6 us -> 66.2 us  [exchange(): return lax.all_to_all(value, axes, 0, 0)]
    ppermute x1, waiting for transfers between devices: 5.08 us -> 0.19 us  [shards(): lax.ppermute(train_rows, panel_axes, forward)]
    pallas_call x1, Pallas kernels: 9.31 us -> 6.52 us  [mean_kernel(): pl.pallas_call(body, out_shape=jax.ShapeDtypeStruct((columns, tests), bf1...]
    ppermute x1, waiting for transfers between devices: 2.38 us -> 0.01 us  [shards(): before = lax.ppermute(weights, panel_axes, forward)]
    pallas_call x3 -> x2, Pallas kernels: 17.1 us -> 15.2 us  [distance_kernel(): pl.pallas_call(distance_body, out_shape=store((slots.shape[0], leaf_size,...]
  transfers between devices with their start and end apart: 7 -> 8, of which waited for: 4 -> 7; matrix products, arithmetic and copies ran while one was open for 0% -> 0% of each run, Pallas kernels for 14% -> 14%
where the time goes in v4:
time: 176 us; the launch traced here: 175 us
  starting transfers between devices  80.1 us (46%)
  Pallas kernels  38.8 us (22%)
  blocking collectives  32.4 us (18%)
  waiting for transfers between devices  19.7 us (11%)
  local copies, waits for them, and re-layouts  3.25 us (2%)
    all_to_all x4, starting transfers between devices, exchange(): return lax.all_to_all(value, axes, 0, 0)  66.2 us
    all_to_all x2, blocking collectives, exchange(): return lax.all_to_all(value, axes, 0, 0)  32.4 us
    pallas_call x8, Pallas kernels, call(): pl.pallas_call(body, out_shape=out_shape, in_specs=specs, out_specs=out_s...  17 us
    all_to_all x4, waiting for transfers between devices, exchange(): return lax.all_to_all(value, axes, 0, 0)  16.5 us
    pallas_call x2, Pallas kernels, distance_kernel(): pl.pallas_call(distance_body, out_shape=store((slots.shape[0], leaf_size,...  15.2 us
    pallas_call x1, Pallas kernels, mean_kernel(): pl.pallas_call(body, out_shape=jax.ShapeDtypeStruct((columns, tests), bf1...  6.52 us
    ppermute x1, starting transfers between devices, shards(): before = lax.ppermute(weights, panel_axes, forward)  3.55 us
  transfers between devices with their start and end apart: 8, of which 7 were waited for; matrix products, arithmetic and copies ran while one was open for 0% of the time, Pallas kernels for 14%

profile of v4, /device:TPU:65, one launch (start us, length us, event | category | flops | bytes accessed | tf_op | source)
XLA Modules:
  0.0 174.7 jit_solution(6929118542897393376)
XLA Ops:
  0.0 0.0 copy-start.7
  0.0 3.6 %mixer.1 = f32[16,32,256]{2,1,0:T(8,128)} custom-call(bf16[320,2048]{1,0:T(8,128)(2,1)} %bitcast.14, f32[10,32,64]{2,1,0:T(8,128)} %bitcast.17), custom_call_target="tpu_custom_call" | custom-call | tf_op jit(solution)/shard_map/mixer/pallas_call | solution.py:49
  3.6 44.9 %all-to-all-start = ((f32[16,32,256]{2,1,0:T(8,128)}), f32[16,32,256]{2,1,0:T(8,128)S(1)}, u32[]{:S(2)}, u32[]{:S(2)}) async-start(f32[16,32,256]{2,1,0:T(8,128)} %mixer.1), calls=%async_computation | async-start | bytes 1048576 | tf_op jit(solution)/shard_map/all_to_all | solution.py:423
  48.6 0.0 copy-start.5
  48.6 0.7 copy-done.5
  49.3 0.0 copy-start.6
  49.3 0.7 copy-done.6
  50.0 0.2 points.1
  50.2 7.8 %local.1 = (f32[64,2048]{1,0:T(8,128)}, f32[64,256]{1,0:T(8,128)}) custom-call(bf16[64,2048]{1,0:T(8,128)(2,1)} %targets_ref.1, s32[1,2048]{1,0:T(1,128)} %order_ref, bf16[4,512,512]{2,1,0:T(8,128)(2,1)} %inverse_ref.1, bf16[320,2048]{1,0:T(8,128)(2,1)} %bitcast.15, f32[10,32,64]{2,1,0:T(8,128)} %bitcast.18), custom_call_target="tpu_custom_call" | custom-call | tf_op jit(solution)/shard_map/local/pallas_call | solution.py:49
  58.0 5.4 %all-to-all-done.refs_1_ = f32[16,32,256]{2,1,0:T(8,128)S(1)} async-done(((f32[16,32,256]{2,1,0:T(8,128)}), f32[16,32,256]{2,1,0:T(8,128)S(1)}, u32[]{:S(2)}, u32[]{:S(2)}) %all-to-all-start) | async-done | bytes 524320 | tf_op jit(solution)/shard_map/all_to_all | solution.py:423
  63.4 0.7 broadcast_in_dim.4
  64.1 7.2 %all-to-all-start.1 = ((f32[16,16,128]{2,1,0:T(8,128)}), f32[16,16,128]{2,1,0:T(8,128)S(1)}, u32[]{:S(2)}, u32[]{:S(2)}) async-start(f32[16,16,128]{2,1,0:T(8,128)} %broadcast_in_dim.4), calls=%async_computation.1 | async-start | bytes 262144 | tf_op jit(solution)/shard_map/all_to_all | solution.py:423
  71.3 0.0 copy-done.7
  71.3 3.5 %collective-permute-start = (bf16[16,2048]{1,0:T(8,128)(2,1)S(1)}, bf16[16,2048]{1,0:T(8,128)(2,1)S(1)}, u32[]{:S(2)}, u32[]{:S(2)}) collective-permute-start(bf16[16,2048]{1,0:T(8,128)(2,1)S(1)} %get-tuple-element.42.mine_ref), channel_id=1, source_target_pairs={{0,1},{1,2},{2,3},{3,4},{4,5},{5,6},{6,7},{7,8},{8,9},{9,10},{10,1... | collective-permute-start | bytes 196616 | tf_op jit(solution)/shard_map/ppermute | solution.py:504
  74.8 3.4 %collective-permute-start.1 = (bf16[16,2048]{1,0:T(8,128)(2,1)S(1)}, bf16[16,2048]{1,0:T(8,128)(2,1)S(1)}, u32[]{:S(2)}, u32[]{:S(2)}) collective-permute-start(bf16[16,2048]{1,0:T(8,128)(2,1)S(1)} %get-tuple-element.42.mine_ref), channel_id=1, source_target_pairs={{1,0},{2,1},{3,2},{4,3},{5,4},{6,5},{7,6},{8,7},{9,8},{10,9},{11,1... | collective-permute-start | bytes 196616 | tf_op jit(solution)/shard_map/ppermute | solution.py:506
  78.2 0.1 pad_add_fusion.refs_0_
  78.2 0.2 collective-permute-done.before_ref
  78.4 1.7 collective-permute-done.1.after_ref
  80.1 2.9 %all-to-all-done.1.refs_2_ = f32[16,16,128]{2,1,0:T(8,128)S(1)} async-done(((f32[16,16,128]{2,1,0:T(8,128)}), f32[16,16,128]{2,1,0:T(8,128)S(1)}, u32[]{:S(2)}, u32[]{:S(2)}) %all-to-all-start.1) | async-done | bytes 131104 | tf_op jit(solution)/shard_map/all_to_all | solution.py:423
  83.0 1.6 operator.1
  84.6 8.3 %all-to-all-start.2 = ((bf16[16,48,256]{2,1,0:T(8,128)(2,1)}), bf16[16,48,256]{2,1,0:T(8,128)(2,1)S(1)}, u32[]{:S(2)}, u32[]{:S(2)}) async-start(bf16[16,48,256]{2,1,0:T(8,128)(2,1)} %operator.1), calls=%async_computation.2 | async-start | bytes 786432 | tf_op jit(solution)/shard_map/all_to_all | solution.py:423
  92.9 0.0 copy-start.4
  92.9 0.0 copy-start
  93.0 0.0 copy-start.1
  93.0 11.5 %near_late.1.refs_4_ = bf16[6,512,2048]{2,1,0:T(8,128)(2,1)} custom-call(s32[6]{0:T(128)S(1)} %slice_bitcast_fusion.1.slots_ref, bf16[16,2048]{1,0:T(8,128)(2,1)S(1)} %collective-permute-done.before_ref, bf16[16,2048]{1,0:T(8,128)(2,1)S(1)} %get-tuple-element.42.mine_ref, bf16[16,2048]{1,0:T(8,128)(2,1)S(1)} %collective-permute-done.1.after_ref, ...), custom_call_target="tpu_custom_call" | custom-call | tf_op jit(solution)/shard_map/near_late/pallas_call | solution.py:168
  104.4 0.0 copy-start.2
  104.5 0.9 all-to-all-done.2.refs_1_
  105.4 0.0 copy-done.4
  105.4 1.1 eliminate.1
  106.5 13.2 %all_to_all.30.refs_1_ = f32[16,4,256]{2,1,0:T(4,128)S(1)} all-to-all(f32[16,4,256]{2,1,0:T(4,128)S(1)} %eliminate.1), channel_id=1, replica_groups=mesh['grp'=2,'z'=16,'core'=2,'sub'=8] {'core','sub'}, dimensions={0} | all-to-all | bytes 131072 | tf_op jit(solution)/shard_map/all_to_all | solution.py:423
  119.7 19.2 %all_to_all.31.refs_2_ = f32[16,4,128]{2,1,0:T(4,128)S(1)} all-to-all(f32[16,4,128]{2,1,0:T(4,128)S(1)} %broadcast_in_dim.5), channel_id=1, replica_groups=mesh['grp'=2,'z'=16,'core'=2,'sub'=8] {'z'}, dimensions={0} | all-to-all | bytes 65536 | tf_op jit(solution)/shard_map/all_to_all | solution.py:423
  138.9 1.2 subtree.1
  140.2 5.8 %all-to-all-start.5 = ((f32[16,8,256]{2,1,0:T(8,128)}), f32[16,8,256]{2,1,0:T(8,128)S(1)}, u32[]{:S(2)}, u32[]{:S(2)}) async-start(f32[16,8,256]{2,1,0:T(8,128)} %subtree.1), calls=%async_computation.5 | async-start | bytes 262144 | tf_op jit(solution)/shard_map/all_to_all | solution.py:423
  145.9 0.1 slice_bitcast_fusion.2.slots_ref
  146.0 7.2 %all-to-all-done.5.refs_0_ = f32[16,8,256]{2,1,0:T(8,128)S(1)} async-done(((f32[16,8,256]{2,1,0:T(8,128)}), f32[16,8,256]{2,1,0:T(8,128)S(1)}, u32[]{:S(2)}, u32[]{:S(2)}) %all-to-all-start.5) | async-done | bytes 131104 | tf_op jit(solution)/shard_map/all_to_all | solution.py:423
  153.2 0.0 copy-done
  153.2 0.0 copy-done.1
  153.2 0.0 copy-start.3
  153.2 1.0 copy-done.3
  154.3 0.8 weights.1
  155.1 3.6 %collective-permute-start.2 = (bf16[64,2048]{1,0:T(8,128)(2,1)S(1)}, bf16[64,2048]{1,0:T(8,128)(2,1)S(1)}, u32[]{:S(2)}, u32[]{:S(2)}) collective-permute-start(bf16[64,2048]{1,0:T(8,128)(2,1)S(1)} %get-tuple-element.49.refs_2_), channel_id=1, source_target_pairs={{0,1},{1,2},{2,3},{3,4},{4,5},{5,6},{6,7},{7,8},{8,9},{9,10},{10,1... | collective-permute-start | bytes 786440 | tf_op jit(solution)/shard_map/ppermute | solution.py:554
  158.7 3.5 %collective-permute-start.3 = (bf16[64,2048]{1,0:T(8,128)(2,1)S(1)}, bf16[64,2048]{1,0:T(8,128)(2,1)S(1)}, u32[]{:S(2)}, u32[]{:S(2)}) collective-permute-start(bf16[64,2048]{1,0:T(8,128)(2,1)S(1)} %get-tuple-element.49.refs_2_), channel_id=1, source_target_pairs={{1,0},{2,1},{3,2},{4,3},{5,4},{6,5},{7,6},{8,7},{9,8},{10,9},{11,1... | collective-permute-start | bytes 786440 | tf_op jit(solution)/shard_map/ppermute | solution.py:555
  162.1 3.7 %near_last.1.refs_5_ = bf16[2,512,2048]{2,1,0:T(8,128)(2,1)S(1)} custom-call(s32[2]{0:T(128)S(1)} %slice_bitcast_fusion.2.slots_ref, bf16[16,2048]{1,0:T(8,128)(2,1)S(1)} %collective-permute-done.before_ref, bf16[16,2048]{1,0:T(8,128)(2,1)S(1)} %get-tuple-element.42.mine_ref, bf16[16,2048]{1,0:T(8,128)(2,1)S(1)} %collective-permute-done.1.after_ref, ...), custom_call_target="tpu_custom_call" | custom-call | tf_op jit(solution)/shard_map/near_last/pallas_call | solution.py:168
  165.9 0.0 copy-done.2
  165.9 0.8 far.1.refs_6_
  166.7 0.0 collective-permute-done.2.refs_1_
  166.7 1.3 collective-permute-done.3.refs_3_
  168.0 6.5 %posterior_mean.1 = bf16[64,2048]{1,0:T(8,128)(2,1)} custom-call(s32[8]{0:T(128)S(1)} %fusion.refs_0_, bf16[64,2048]{1,0:T(8,128)(2,1)S(1)} %collective-permute-done.2.refs_1_, bf16[64,2048]{1,0:T(8,128)(2,1)S(1)} %get-tuple-element.49.refs_2_, bf16[64,2048]{1,0:T(8,128)(2,1)S(1)} %collective-permute-done.3.refs_3_, bf16[6,512,2048]{2,1,0:T(8,128)(2,1)} %near_late.1.refs_4_, ...), custom_call_target="tpu_custom_call" | custom-call | tf_op jit(solution)/shard_map/posterior_mean/pallas_call | solution.py:395
  (8 shorter events, 0.1 us)
Async XLA Ops:
  0.0 71.3 %copy-start.7 = (s32[1,8]{1,0:T(1,128)S(1)}, s32[1,8]{1,0:T(1,128)}, u32[]{:S(2)}) copy-start(s32[1,8]{1,0:T(1,128)} %param.17) | copy-start | bytes 100
  3.6 59.7 %all-to-all-start = ((f32[16,32,256]{2,1,0:T(8,128)}), f32[16,32,256]{2,1,0:T(8,128)S(1)}, u32[]{:S(2)}, u32[]{:S(2)}) async-start(f32[16,32,256]{2,1,0:T(8,128)} %mixer.1), calls=%async_computation | async-start | bytes 1048576 | tf_op jit(solution)/shard_map/all_to_all | solution.py:423
  48.6 0.7 copy-start.5
  49.3 0.7 copy-start.6
  64.1 19.0 %all-to-all-start.1 = ((f32[16,16,128]{2,1,0:T(8,128)}), f32[16,16,128]{2,1,0:T(8,128)S(1)}, u32[]{:S(2)}, u32[]{:S(2)}) async-start(f32[16,16,128]{2,1,0:T(8,128)} %broadcast_in_dim.4), calls=%async_computation.1 | async-start | bytes 262144 | tf_op jit(solution)/shard_map/all_to_all | solution.py:423
  71.3 7.1 %collective-permute-start = (bf16[16,2048]{1,0:T(8,128)(2,1)S(1)}, bf16[16,2048]{1,0:T(8,128)(2,1)S(1)}, u32[]{:S(2)}, u32[]{:S(2)}) collective-permute-start(bf16[16,2048]{1,0:T(8,128)(2,1)S(1)} %get-tuple-element.42.mine_ref), channel_id=1, source_target_pairs={{0,1},{1,2},{2,3},{3,4},{4,5},{5,6},{6,7},{7,8},{8,9},{9,10},{10,1... | collective-permute-start | bytes 196616 | tf_op jit(solution)/shard_map/ppermute | solution.py:504
  74.8 5.3 %collective-permute-start.1 = (bf16[16,2048]{1,0:T(8,128)(2,1)S(1)}, bf16[16,2048]{1,0:T(8,128)(2,1)S(1)}, u32[]{:S(2)}, u32[]{:S(2)}) collective-permute-start(bf16[16,2048]{1,0:T(8,128)(2,1)S(1)} %get-tuple-element.42.mine_ref), channel_id=1, source_target_pairs={{1,0},{2,1},{3,2},{4,3},{5,4},{6,5},{7,6},{8,7},{9,8},{10,9},{11,1... | collective-permute-start | bytes 196616 | tf_op jit(solution)/shard_map/ppermute | solution.py:506
  84.6 20.8 %all-to-all-start.2 = ((bf16[16,48,256]{2,1,0:T(8,128)(2,1)}), bf16[16,48,256]{2,1,0:T(8,128)(2,1)S(1)}, u32[]{:S(2)}, u32[]{:S(2)}) async-start(bf16[16,48,256]{2,1,0:T(8,128)(2,1)} %operator.1), calls=%async_computation.2 | async-start | bytes 786432 | tf_op jit(solution)/shard_map/all_to_all | solution.py:423
  92.9 12.5 %copy-start.4 = (f32[64,256]{1,0:T(8,128)S(1)}, f32[64,256]{1,0:T(8,128)}, u32[]{:S(2)}) copy-start(f32[64,256]{1,0:T(8,128)} %get-tuple-element.34.refs_0_) | copy-start | bytes 196612
  92.9 60.3 %copy-start = (bf16[10,32,2048]{2,1,0:T(8,128)(2,1)S(1)}, bf16[10,32,2048]{2,1,0:T(8,128)(2,1)}, u32[]{:S(2)}) copy-start(bf16[10,32,2048]{2,1,0:T(8,128)(2,1)} %param.12) | copy-start | bytes 3932164
  93.0 60.3 %copy-start.1 = (f32[1,10,32,64]{3,2,1,0:T(8,128)S(1)}, f32[1,10,32,64]{3,2,1,0:T(8,128)}, u32[]{:S(2)}) copy-start(f32[1,10,32,64]{3,2,1,0:T(8,128)} %param.13) | copy-start | bytes 245764
  104.4 61.4 %copy-start.2 = (bf16[8,32,2048]{2,1,0:T(8,128)(2,1)S(1)}, bf16[8,32,2048]{2,1,0:T(8,128)(2,1)}, u32[]{:S(2)}) copy-start(bf16[8,32,2048]{2,1,0:T(8,128)(2,1)} %param.16) | copy-start | bytes 3145732
  140.2 13.1 %all-to-all-start.5 = ((f32[16,8,256]{2,1,0:T(8,128)}), f32[16,8,256]{2,1,0:T(8,128)S(1)}, u32[]{:S(2)}, u32[]{:S(2)}) async-start(f32[16,8,256]{2,1,0:T(8,128)} %subtree.1), calls=%async_computation.5 | async-start | bytes 262144 | tf_op jit(solution)/shard_map/all_to_all | solution.py:423
  153.2 1.0 copy-start.3
  155.1 11.6 %collective-permute-start.2 = (bf16[64,2048]{1,0:T(8,128)(2,1)S(1)}, bf16[64,2048]{1,0:T(8,128)(2,1)S(1)}, u32[]{:S(2)}, u32[]{:S(2)}) collective-permute-start(bf16[64,2048]{1,0:T(8,128)(2,1)S(1)} %get-tuple-element.49.refs_2_), channel_id=1, source_target_pairs={{0,1},{1,2},{2,3},{3,4},{4,5},{5,6},{6,7},{7,8},{8,9},{9,10},{10,1... | collective-permute-start | bytes 786440 | tf_op jit(solution)/shard_map/ppermute | solution.py:554
  158.7 9.4 %collective-permute-start.3 = (bf16[64,2048]{1,0:T(8,128)(2,1)S(1)}, bf16[64,2048]{1,0:T(8,128)(2,1)S(1)}, u32[]{:S(2)}, u32[]{:S(2)}) collective-permute-start(bf16[64,2048]{1,0:T(8,128)(2,1)S(1)} %get-tuple-element.49.refs_2_), channel_id=1, source_target_pairs={{1,0},{2,1},{3,2},{4,3},{5,4},{6,5},{7,6},{8,7},{9,8},{10,9},{11,1... | collective-permute-start | bytes 786440 | tf_op jit(solution)/shard_map/ppermute | solution.py:555

commit v5 on v4

--- a/solution.py
+++ b/solution.py
@@ -139,8 +139,10 @@
     )
 
 
-def distance_body(slots_ref, before_ref, mine_ref, after_ref, test_ref, out_ref, train_ref):
-    leaf = slots_ref[pl.program_id(0)]
+def distance_body(
+    slots_ref, before_ref, mine_ref, after_ref, test_ref, out_ref, train_ref, *, first
+):
+    leaf = slots_ref[first + pl.program_id(0)]
     leaf_size = train_ref.shape[1]
     leaf_count = mine_ref.shape[1] // leaf_size
     for side, ref in enumerate((before_ref, mine_ref, after_ref)):
@@ -162,15 +164,19 @@
         out_ref[0, :, start : start + step] = ((1.0 + scaled) * jnp.exp(-scaled)).astype(bf16)
 
 
-def distance_kernel(slots, sides, test_features, leaf_size, name, store):
+def distance_kernel(slots, first, count, sides, test_features, leaf_size, name, store):
     tests = test_features.shape[1]
     operands = (*sides, test_features)
+
+    def body(*refs):
+        distance_body(*refs, first=first)
+
     return pl.pallas_call(
-        distance_body,
-        out_shape=store((slots.shape[0], leaf_size, tests), bf16),
+        body,
+        out_shape=store((count, leaf_size, tests), bf16),
         grid_spec=pltpu.PrefetchScalarGridSpec(
             num_scalar_prefetch=1,
-            grid=(slots.shape[0],),
+            grid=(count,),
             in_specs=[pl.BlockSpec(a.shape, lambda i, s: (0, 0)) for a in operands],
             out_specs=pl.BlockSpec((1, leaf_size, tests), lambda i, s: (i, 0, 0)),
             scratch_shapes=[pltpu.VMEM((sides[0].shape[0], leaf_size), bf16)],
@@ -514,9 +520,11 @@
     operators = whole_call(
         operator, jax.ShapeDtypeStruct((low_count, 3 * part, width), bf16), "operator", 1
     )(place, spread, high_spread)
-    late_slots, operators = tie(slots[:stored], operators)
+    late_rows, operators = tie(test_rows, operators)
     operators = exchange(operators, low_axes)
-    late = distance_kernel(late_slots, sides, test_rows, leaf_size, "near_late", pltpu.HBM)
+    late = distance_kernel(
+        slots, 0, stored, sides, late_rows, leaf_size, "near_late", pltpu.HBM
+    )
     late, operators = tie(late, operators)
 
     def eliminate(*refs):
@@ -547,9 +555,9 @@
         ],
         "weights",
     )(sums, state, basis, mixers)
-    last_slots, weights = tie(slots[stored:], weights)
+    last_rows, weights = tie(test_rows, weights)
     last = distance_kernel(
-        last_slots, sides, test_rows, leaf_size, "near_last", jax.ShapeDtypeStruct
+        slots, stored, last_count, sides, last_rows, leaf_size, "near_last", jax.ShapeDtypeStruct
     )
     before = lax.ppermute(weights, panel_axes, forward)
     after = lax.ppermute(weights, panel_axes, backward)

time: 176 us -> 176 us (level)
  blocking collectives: 32.4 us -> 45.9 us
  waiting for transfers between devices: 19.7 us -> 11.8 us
  starting transfers between devices: 80.1 us -> 73.2 us
  local copies, waits for them, and re-layouts: 3.25 us -> 5.51 us
    all_to_all x2 -> x3, blocking collectives: 32.4 us -> 45.9 us  [exchange(): return lax.all_to_all(value, axes, 0, 0)]
    all_to_all x4 -> x3, waiting for transfers between devices: 16.5 us -> 6.73 us  [exchange(): return lax.all_to_all(value, axes, 0, 0)]
    all_to_all x4 -> x3, starting transfers between devices: 66.2 us -> 60.6 us  [exchange(): return lax.all_to_all(value, axes, 0, 0)]
    ppermute x1, waiting for transfers between devices: 0.19 us -> 5.08 us  [shards(): lax.ppermute(train_rows, panel_axes, forward)]
    unnamed x16 -> x32, local copies, waits for them, and re-layouts: 2.49 us -> 4.82 us
  transfers between devices with their start and end apart: 8 -> 7, of which waited for: 7 -> 4; matrix products, arithmetic and copies ran while one was open for 0% -> 0% of each run, Pallas kernels for 14% -> 14%
where the time goes in v5:
time: 176 us; the launch traced here: 175 us
  starting transfers between devices  73.2 us (42%)
  blocking collectives  45.9 us (26%)
  Pallas kernels  38.2 us (22%)
  waiting for transfers between devices  11.8 us (7%)
  local copies, waits for them, and re-layouts  5.51 us (3%)
    all_to_all x3, starting transfers between devices, exchange(): return lax.all_to_all(value, axes, 0, 0)  60.6 us
    all_to_all x3, blocking collectives, exchange(): return lax.all_to_all(value, axes, 0, 0)  45.9 us
    pallas_call x8, Pallas kernels, call(): pl.pallas_call(body, out_shape=out_shape, in_specs=specs, out_specs=out_s...  16.4 us
    pallas_call x2, Pallas kernels, distance_kernel(): pl.pallas_call(body, out_shape=store((count, leaf_size, tests), bf16), gr...  15.2 us
    all_to_all x3, waiting for transfers between devices, exchange(): return lax.all_to_all(value, axes, 0, 0)  6.73 us
    pallas_call x1, Pallas kernels, mean_kernel(): pl.pallas_call(body, out_shape=jax.ShapeDtypeStruct((columns, tests), bf1...  6.52 us
    ppermute x1, waiting for transfers between devices, shards(): lax.ppermute(train_rows, panel_axes, forward)  5.08 us
    unnamed x32, local copies, waits for them, and re-layouts  4.82 us
  transfers between devices with their start and end apart: 7, of which 4 were waited for; matrix products, arithmetic and copies ran while one was open for 0% of the time, Pallas kernels for 14%

profile of v5, /device:TPU:65, one launch (start us, length us, event | category | flops | bytes accessed | tf_op | source)
XLA Modules:
  0.0 175.2 jit_solution(502817105455493924)
XLA Ops:
  0.0 3.6 %mixer.1 = f32[16,32,256]{2,1,0:T(8,128)} custom-call(bf16[320,2048]{1,0:T(8,128)(2,1)} %bitcast.10, f32[10,32,64]{2,1,0:T(8,128)} %bitcast.13), custom_call_target="tpu_custom_call" | custom-call | tf_op jit(solution)/shard_map/mixer/pallas_call | solution.py:49
  3.6 45.1 %all-to-all-start = ((f32[16,32,256]{2,1,0:T(8,128)}), f32[16,32,256]{2,1,0:T(8,128)S(1)}, u32[]{:S(2)}, u32[]{:S(2)}) async-start(f32[16,32,256]{2,1,0:T(8,128)} %mixer.1), calls=%async_computation | async-start | bytes 1048576 | tf_op jit(solution)/shard_map/all_to_all | solution.py:429
  48.7 0.7 copy-done.13
  49.4 0.7 copy-done.14
  50.1 0.2 points.1
  50.3 0.0 copy-start.4
  50.3 0.0 copy-start.6
  50.3 7.8 %local.1 = (f32[64,2048]{1,0:T(8,128)}, f32[64,256]{1,0:T(8,128)}) custom-call(bf16[64,2048]{1,0:T(8,128)(2,1)} %targets_ref.1, s32[1,2048]{1,0:T(1,128)} %order_ref, bf16[4,512,512]{2,1,0:T(8,128)(2,1)} %inverse_ref.1, bf16[320,2048]{1,0:T(8,128)(2,1)} %bitcast.11, f32[10,32,64]{2,1,0:T(8,128)} %bitcast.14), custom_call_target="tpu_custom_call" | custom-call | tf_op jit(solution)/shard_map/local/pallas_call | solution.py:49
  58.1 5.4 %all-to-all-done.refs_1_ = f32[16,32,256]{2,1,0:T(8,128)S(1)} async-done(((f32[16,32,256]{2,1,0:T(8,128)}), f32[16,32,256]{2,1,0:T(8,128)S(1)}, u32[]{:S(2)}, u32[]{:S(2)}) %all-to-all-start) | async-done | bytes 524320 | tf_op jit(solution)/shard_map/all_to_all | solution.py:429
  63.5 0.7 broadcast_in_dim.4
  64.2 7.2 %all-to-all-start.1 = ((f32[16,16,128]{2,1,0:T(8,128)}), f32[16,16,128]{2,1,0:T(8,128)S(1)}, u32[]{:S(2)}, u32[]{:S(2)}) async-start(f32[16,16,128]{2,1,0:T(8,128)} %broadcast_in_dim.4), calls=%async_computation.1 | async-start | bytes 262144 | tf_op jit(solution)/shard_map/all_to_all | solution.py:429
  71.4 4.1 %collective-permute-start.1 = (bf16[16,2048]{1,0:T(8,128)(2,1)S(1)}, bf16[16,2048]{1,0:T(8,128)(2,1)S(1)}, u32[]{:S(2)}, u32[]{:S(2)}) collective-permute-start(bf16[16,2048]{1,0:T(8,128)(2,1)S(1)} %get-tuple-element.41.refs_2_), channel_id=1, source_target_pairs={{1,0},{2,1},{3,2},{4,3},{5,4},{6,5},{7,6},{8,7},{9,8},{10,9},{11,1... | collective-permute-start | bytes 196616 | tf_op jit(solution)/shard_map/ppermute | solution.py:512
  75.5 2.0 %collective-permute-start = (bf16[16,2048]{1,0:T(8,128)(2,1)S(1)}, bf16[16,2048]{1,0:T(8,128)(2,1)S(1)}, u32[]{:S(2)}, u32[]{:S(2)}) collective-permute-start(bf16[16,2048]{1,0:T(8,128)(2,1)S(1)} %get-tuple-element.41.refs_2_), channel_id=1, source_target_pairs={{0,1},{1,2},{2,3},{3,4},{4,5},{5,6},{6,7},{7,8},{8,9},{9,10},{10,1... | collective-permute-start | bytes 196616 | tf_op jit(solution)/shard_map/ppermute | solution.py:510
  77.5 0.1 pad_add_fusion.refs_0_
  77.6 0.0 collective-permute-done.1.refs_3_
  77.6 5.1 %collective-permute-done.refs_1_ = bf16[16,2048]{1,0:T(8,128)(2,1)S(1)} collective-permute-done((bf16[16,2048]{1,0:T(8,128)(2,1)S(1)}, bf16[16,2048]{1,0:T(8,128)(2,1)S(1)}, u32[]{:S(2)}, u32[]{:S(2)}) %collective-permute-start) | collective-permute-done | bytes 65568 | tf_op jit(solution)/shard_map/ppermute | solution.py:510
  82.7 0.5 all-to-all-done.1.refs_2_
  83.2 1.6 operator.1
  84.7 8.3 %all-to-all-start.2 = ((bf16[16,48,256]{2,1,0:T(8,128)(2,1)}), bf16[16,48,256]{2,1,0:T(8,128)(2,1)S(1)}, u32[]{:S(2)}, u32[]{:S(2)}) async-start(bf16[16,48,256]{2,1,0:T(8,128)(2,1)} %operator.1), calls=%async_computation.2 | async-start | bytes 786432 | tf_op jit(solution)/shard_map/all_to_all | solution.py:429
  93.1 0.0 copy-done.15
  93.1 0.0 copy-done.4
  93.1 0.0 copy-done.6
  93.1 0.0 copy-done.8
  93.1 0.0 copy-done.10
  93.1 0.0 copy-start.12
  93.1 0.0 copy-start
  93.1 0.0 copy-start.1
  93.1 0.0 copy-start.3
  93.2 11.5 %near_late.1.refs_4_ = bf16[6,512,2048]{2,1,0:T(8,128)(2,1)} custom-call(s32[8]{0:T(128)S(1)} %subtract_bitcast_fusion.refs_0_, bf16[16,2048]{1,0:T(8,128)(2,1)S(1)} %collective-permute-done.refs_1_, bf16[16,2048]{1,0:T(8,128)(2,1)S(1)} %get-tuple-element.41.refs_2_, bf16[16,2048]{1,0:T(8,128)(2,1)S(1)} %collective-permute-done.1.refs_3_, ...), custom_call_target="tpu_custom_call" | custom-call | tf_op jit(solution)/shard_map/near_late/pallas_call | solution.py:174
  104.6 0.9 all-to-all-done.2.refs_1_
  105.5 0.0 copy-done.12
  105.5 1.1 eliminate.1
  106.6 13.3 %all_to_all.30.refs_1_ = f32[16,4,256]{2,1,0:T(4,128)S(1)} all-to-all(f32[16,4,256]{2,1,0:T(4,128)S(1)} %eliminate.1), channel_id=1, replica_groups=mesh['grp'=2,'z'=16,'core'=2,'sub'=8] {'core','sub'}, dimensions={0} | all-to-all | bytes 131072 | tf_op jit(solution)/shard_map/all_to_all | solution.py:429
  119.9 20.5 %all_to_all.31.refs_2_ = f32[16,4,128]{2,1,0:T(4,128)S(1)} all-to-all(f32[16,4,128]{2,1,0:T(4,128)S(1)} %broadcast_in_dim.5), channel_id=1, replica_groups=mesh['grp'=2,'z'=16,'core'=2,'sub'=8] {'z'}, dimensions={0} | all-to-all | bytes 65536 | tf_op jit(solution)/shard_map/all_to_all | solution.py:429
  140.4 0.6 subtree.1
  141.0 12.2 %all_to_all.32.refs_0_ = f32[16,8,256]{2,1,0:T(8,128)S(1)} all-to-all(f32[16,8,256]{2,1,0:T(8,128)S(1)} %subtree.1), channel_id=1, replica_groups=mesh['grp'=2,'z'=16,'core'=2,'sub'=8] {'core','sub'}, dimensions={0} | all-to-all | bytes 262144 | tf_op jit(solution)/shard_map/all_to_all | solution.py:429
  153.1 0.8 weights.1
  154.0 4.4 %collective-permute-start.3 = (bf16[64,2048]{1,0:T(8,128)(2,1)S(1)}, bf16[64,2048]{1,0:T(8,128)(2,1)S(1)}, u32[]{:S(2)}, u32[]{:S(2)}) collective-permute-start(bf16[64,2048]{1,0:T(8,128)(2,1)S(1)} %get-tuple-element.49.refs_2_), channel_id=1, source_target_pairs={{1,0},{2,1},{3,2},{4,3},{5,4},{6,5},{7,6},{8,7},{9,8},{10,9},{11,1... | collective-permute-start | bytes 786440 | tf_op jit(solution)/shard_map/ppermute | solution.py:563
  158.4 2.1 %collective-permute-start.2 = (bf16[64,2048]{1,0:T(8,128)(2,1)S(1)}, bf16[64,2048]{1,0:T(8,128)(2,1)S(1)}, u32[]{:S(2)}, u32[]{:S(2)}) collective-permute-start(bf16[64,2048]{1,0:T(8,128)(2,1)S(1)} %get-tuple-element.49.refs_2_), channel_id=1, source_target_pairs={{0,1},{1,2},{2,3},{3,4},{4,5},{5,6},{6,7},{7,8},{8,9},{9,10},{10,1... | collective-permute-start | bytes 786440 | tf_op jit(solution)/shard_map/ppermute | solution.py:562
  160.5 0.8 copy-done.5
  161.4 0.8 copy-done.7
  162.2 0.8 copy-done.9
  163.1 0.8 copy-done.11
  163.9 3.7 %near_last.1.refs_5_ = bf16[2,512,2048]{2,1,0:T(8,128)(2,1)S(1)} custom-call(s32[8]{0:T(128)S(1)} %subtract_bitcast_fusion.refs_0_, bf16[16,2048]{1,0:T(8,128)(2,1)S(1)} %copy-done.11, bf16[16,2048]{1,0:T(8,128)(2,1)S(1)} %copy-done.5, bf16[16,2048]{1,0:T(8,128)(2,1)S(1)} %copy-done.9, bf16[16,2048]{1,0:T(8,128)(2,1)S(1)} %copy-done.7), custom_call_target="tpu_custom_call" | custom-call | tf_op jit(solution)/shard_map/near_last/pallas_call | solution.py:174
  167.7 0.8 far.1.refs_6_
  168.5 0.0 collective-permute-done.3.refs_3_
  168.5 0.0 collective-permute-done.2.refs_1_
  168.5 6.5 %posterior_mean.1 = bf16[64,2048]{1,0:T(8,128)(2,1)} custom-call(s32[8]{0:T(128)S(1)} %subtract_bitcast_fusion.refs_0_, bf16[64,2048]{1,0:T(8,128)(2,1)S(1)} %collective-permute-done.2.refs_1_, bf16[64,2048]{1,0:T(8,128)(2,1)S(1)} %get-tuple-element.49.refs_2_, bf16[64,2048]{1,0:T(8,128)(2,1)S(1)} %collective-permute-done.3.refs_3_, ...), custom_call_target="tpu_custom_call" | custom-call | tf_op jit(solution)/shard_map/posterior_mean/pallas_call | solution.py:401
  (20 shorter events, 0.1 us)
Async XLA Ops:
  3.6 89.4 %copy-start.15 = (s32[1,8]{1,0:T(1,128)S(1)}, s32[1,8]{1,0:T(1,128)}, u32[]{:S(2)}) copy-start(s32[1,8]{1,0:T(1,128)} %param.17) | copy-start | bytes 100
  3.6 59.9 %all-to-all-start = ((f32[16,32,256]{2,1,0:T(8,128)}), f32[16,32,256]{2,1,0:T(8,128)S(1)}, u32[]{:S(2)}, u32[]{:S(2)}) async-start(f32[16,32,256]{2,1,0:T(8,128)} %mixer.1), calls=%async_computation | async-start | bytes 1048576 | tf_op jit(solution)/shard_map/all_to_all | solution.py:429
  48.7 0.7 copy-start.13
  49.4 0.7 copy-start.14
  50.3 42.8 %copy-start.4 = (bf16[16,2048]{1,0:T(8,128)(2,1)}, bf16[16,2048]{1,0:T(8,128)(2,1)S(1)}, u32[]{:S(2)}) copy-start(bf16[16,2048]{1,0:T(8,128)(2,1)S(1)} %get-tuple-element.41.refs_2_) | copy-start | bytes 196612
  50.3 42.8 %copy-start.6 = (bf16[16,2048]{1,0:T(8,128)(2,1)}, bf16[16,2048]{1,0:T(8,128)(2,1)S(1)}, u32[]{:S(2)}) copy-start(bf16[16,2048]{1,0:T(8,128)(2,1)S(1)} %get-tuple-element.51.refs_4_) | copy-start | bytes 196612
  64.2 19.0 %all-to-all-start.1 = ((f32[16,16,128]{2,1,0:T(8,128)}), f32[16,16,128]{2,1,0:T(8,128)S(1)}, u32[]{:S(2)}, u32[]{:S(2)}) async-start(f32[16,16,128]{2,1,0:T(8,128)} %broadcast_in_dim.4), calls=%async_computation.1 | async-start | bytes 262144 | tf_op jit(solution)/shard_map/all_to_all | solution.py:429
  71.4 6.2 %collective-permute-start.1 = (bf16[16,2048]{1,0:T(8,128)(2,1)S(1)}, bf16[16,2048]{1,0:T(8,128)(2,1)S(1)}, u32[]{:S(2)}, u32[]{:S(2)}) collective-permute-start(bf16[16,2048]{1,0:T(8,128)(2,1)S(1)} %get-tuple-element.41.refs_2_), channel_id=1, source_target_pairs={{1,0},{2,1},{3,2},{4,3},{5,4},{6,5},{7,6},{8,7},{9,8},{10,9},{11,1... | collective-permute-start | bytes 196616 | tf_op jit(solution)/shard_map/ppermute | solution.py:512
  75.5 7.1 %collective-permute-start = (bf16[16,2048]{1,0:T(8,128)(2,1)S(1)}, bf16[16,2048]{1,0:T(8,128)(2,1)S(1)}, u32[]{:S(2)}, u32[]{:S(2)}) collective-permute-start(bf16[16,2048]{1,0:T(8,128)(2,1)S(1)} %get-tuple-element.41.refs_2_), channel_id=1, source_target_pairs={{0,1},{1,2},{2,3},{3,4},{4,5},{5,6},{6,7},{7,8},{8,9},{9,10},{10,1... | collective-permute-start | bytes 196616 | tf_op jit(solution)/shard_map/ppermute | solution.py:510
  77.6 15.5 %copy-start.8 = (bf16[16,2048]{1,0:T(8,128)(2,1)}, bf16[16,2048]{1,0:T(8,128)(2,1)S(1)}, u32[]{:S(2)}) copy-start(bf16[16,2048]{1,0:T(8,128)(2,1)S(1)} %collective-permute-done.1.refs_3_) | copy-start | bytes 196612
  82.7 10.4 %copy-start.10 = (bf16[16,2048]{1,0:T(8,128)(2,1)}, bf16[16,2048]{1,0:T(8,128)(2,1)S(1)}, u32[]{:S(2)}) copy-start(bf16[16,2048]{1,0:T(8,128)(2,1)S(1)} %collective-permute-done.refs_1_) | copy-start | bytes 196612
  84.7 20.8 %all-to-all-start.2 = ((bf16[16,48,256]{2,1,0:T(8,128)(2,1)}), bf16[16,48,256]{2,1,0:T(8,128)(2,1)S(1)}, u32[]{:S(2)}, u32[]{:S(2)}) async-start(bf16[16,48,256]{2,1,0:T(8,128)(2,1)} %operator.1), calls=%async_computation.2 | async-start | bytes 786432 | tf_op jit(solution)/shard_map/all_to_all | solution.py:429
  93.1 12.4 %copy-start.12 = (f32[64,256]{1,0:T(8,128)S(1)}, f32[64,256]{1,0:T(8,128)}, u32[]{:S(2)}) copy-start(f32[64,256]{1,0:T(8,128)} %get-tuple-element.35.refs_0_) | copy-start | bytes 196612
  93.1 60.0 %copy-start = (bf16[10,32,2048]{2,1,0:T(8,128)(2,1)S(1)}, bf16[10,32,2048]{2,1,0:T(8,128)(2,1)}, u32[]{:S(2)}) copy-start(bf16[10,32,2048]{2,1,0:T(8,128)(2,1)} %param.12) | copy-start | bytes 3932164
  93.1 60.0 %copy-start.1 = (f32[1,10,32,64]{3,2,1,0:T(8,128)S(1)}, f32[1,10,32,64]{3,2,1,0:T(8,128)}, u32[]{:S(2)}) copy-start(f32[1,10,32,64]{3,2,1,0:T(8,128)} %param.13) | copy-start | bytes 245764
  93.1 60.0 %copy-start.3 = (f32[64,2048]{1,0:T(8,128)S(1)}, f32[64,2048]{1,0:T(8,128)}, u32[]{:S(2)}) copy-start(f32[64,2048]{1,0:T(8,128)} %get-tuple-element.47.refs_1_) | copy-start | bytes 1572868
  104.6 63.0 %copy-start.2 = (bf16[8,32,2048]{2,1,0:T(8,128)(2,1)S(1)}, bf16[8,32,2048]{2,1,0:T(8,128)(2,1)}, u32[]{:S(2)}) copy-start(bf16[8,32,2048]{2,1,0:T(8,128)(2,1)} %param.16) | copy-start | bytes 3145732
  154.0 14.5 %collective-permute-start.3 = (bf16[64,2048]{1,0:T(8,128)(2,1)S(1)}, bf16[64,2048]{1,0:T(8,128)(2,1)S(1)}, u32[]{:S(2)}, u32[]{:S(2)}) collective-permute-start(bf16[64,2048]{1,0:T(8,128)(2,1)S(1)} %get-tuple-element.49.refs_2_), channel_id=1, source_target_pairs={{1,0},{2,1},{3,2},{4,3},{5,4},{6,5},{7,6},{8,7},{9,8},{10,9},{11,1... | collective-permute-start | bytes 786440 | tf_op jit(solution)/shard_map/ppermute | solution.py:563
  158.4 10.1 %collective-permute-start.2 = (bf16[64,2048]{1,0:T(8,128)(2,1)S(1)}, bf16[64,2048]{1,0:T(8,128)(2,1)S(1)}, u32[]{:S(2)}, u32[]{:S(2)}) collective-permute-start(bf16[64,2048]{1,0:T(8,128)(2,1)S(1)} %get-tuple-element.49.refs_2_), channel_id=1, source_target_pairs={{0,1},{1,2},{2,3},{3,4},{4,5},{5,6},{6,7},{7,8},{8,9},{9,10},{10,1... | collective-permute-start | bytes 786440 | tf_op jit(solution)/shard_map/ppermute | solution.py:562
  160.5 0.8 copy-start.5
  161.4 0.8 copy-start.7
  162.2 0.8 copy-start.9
  163.1 0.8 copy-start.11
